TPU v7x, 256 devices: a whole 4x4x8 slice. The times are simulated.
256 devices in a mesh: space: 32 (over y, z_hi, core), filt: 8 (over z_lo, x).
Axes of the slice: x: 4, y: 4, z: 8 (z_hi: 4, z_lo: 2; z = z_hi * 2 + z_lo), core: 2. Of those that a mesh axis runs over, the one named last changes fastest.
Arguments:
- volume: bfloat16 [64, 64, 16, 256], P(None, 'space', 'filt'), may hold values from -6 to 6
- first_weight: bfloat16 [27, 64, 64], replicated, may hold values from -0.15625 to 0.15625
- second_weight: bfloat16 [27, 128, 64], P(None, 'filt'), may hold values from -0.15625 to 0.15625
- cotangent: bfloat16 [128, 32, 8, 128], P('filt', 'space'), may hold values from -24 to 24
Outputs:
- features: bfloat16 [128, 32, 8, 128], P('filt', 'space')
- volume_grad: bfloat16 [64, 64, 16, 256], P(None, 'space', 'filt')
- first_grad: float32 [27, 64, 64], replicated
- second_grad: float32 [27, 128, 64], P(None, 'filt')
All inputs are finite; a program needn't handle non-finite values.
Results may differ from a plain program's by a relative error of at most 0.019.
Values may be sent and summed in bfloat16 or wider, within the bound.
A program may use at most 64 MiB of HBM per device.

v0:
```python
import jax
import jax.numpy as jnp
from jax import lax
from jax.sharding import PartitionSpec as P


def extended(cells, sides, width):
    for axis, dim in sides:
        count = lax.axis_size(axis)
        ends = count - 1
        head = lax.slice_in_dim(cells, 0, width, axis=dim)
        tail = lax.slice_in_dim(cells, cells.shape[dim] - width, cells.shape[dim], axis=dim)
        cells = jnp.concatenate(
            [
                lax.ppermute(tail, axis, [(i, (i + 1) % count) for i in range(ends)]),
                cells,
                lax.ppermute(head, axis, [((i + 1) % count, i) for i in range(ends)]),
            ],
            axis=dim,
        )
    return cells


def from_everyone(value, axis):
    copies = jnp.broadcast_to(value, (lax.axis_size(axis), *value.shape))
    return lax.all_to_all(copies, axis, split_axis=0, concat_axis=0, tiled=True)


def laid_out(tiles, dim):
    lengths = list(tiles.shape[1:])
    lengths[dim] *= tiles.shape[0]
    return jnp.moveaxis(tiles, 0, dim).reshape(lengths)


def collect(value, axis, dim):
    tiles = from_everyone(value, axis)
    return laid_out(tiles, dim)


def total_of_pieces(value, axis):
    tiles = lax.all_gather(value, axis).astype(jnp.float32)
    return tiles.sum(axis=0)


def in_blocks(value, dim, devices):
    before, after = (value.shape[:dim], value.shape[dim + 1 :])
    return jnp.moveaxis(value.reshape(*before, devices, -1, *after), dim, 0)


def sum_at_owner(value, axis, dim):
    devices = lax.axis_size(axis)
    tiles = lax.all_to_all(in_blocks(value, dim, devices), axis, 0, 0, tiled=True)
    return jnp.sum(tiles.astype(jnp.float32), axis=0)


def silu_slope(values):
    sigmoid_part = jax.nn.sigmoid(values)
    return sigmoid_part * (1.0 + values * (1.0 - sigmoid_part))


def pad_depth(volume_field):
    return jnp.pad(volume_field, ((0, 0), (0, 0), (0, 0), (1, 1)))


def window(padded, offset_x, offset_y, offset_z, extents):
    extent_x, extent_y, extent_z = extents
    section = lax.slice(
        padded,
        (0, offset_x, offset_y, offset_z),
        (padded.shape[0], offset_x + extent_x, offset_y + extent_y, offset_z + extent_z),
    )
    return section.reshape(padded.shape[0], extent_x * extent_y * extent_z)


def conv_forward(padded, weight, extents):
    outputs, inputs = (weight.shape[1], weight.shape[2])
    running = jnp.zeros((outputs, extents[0] * extents[1] * extents[2]), jnp.float32)
    for offset_x in range(3):
        for offset_y in range(3):
            tap_base = offset_x * 9 + offset_y * 3
            stacked = jnp.concatenate(
                [window(padded, offset_x, offset_y, offset_z, extents) for offset_z in range(3)],
                axis=0,
            )
            matrices = jnp.transpose(weight[tap_base : tap_base + 3], (1, 0, 2)).reshape(
                outputs, 3 * inputs
            )
            running = running + jnp.dot(matrices, stacked, preferred_element_type=jnp.float32)
    return running


def conv_transpose(padded, weight, extents):
    outputs, inputs = (weight.shape[1], weight.shape[2])
    running = jnp.zeros((inputs, extents[0] * extents[1] * extents[2]), jnp.float32)
    for offset_x in range(3):
        for offset_y in range(3):
            tap_base = offset_x * 9 + offset_y * 3
            stacked = jnp.concatenate(
                [window(padded, offset_x, offset_y, offset_z, extents) for offset_z in range(3)],
                axis=0,
            )
            tap_block = weight[24 - tap_base : 27 - tap_base][::-1]
            matrices = jnp.transpose(tap_block, (2, 0, 1)).reshape(inputs, 3 * outputs)
            running = running + jnp.dot(matrices, stacked, preferred_element_type=jnp.float32)
    return running


def conv_weights(grad_rows, padded, extents):
    outputs, inputs = (grad_rows.shape[0], padded.shape[0])
    blocks = []
    for offset_x in range(3):
        for offset_y in range(3):
            stacked = jnp.concatenate(
                [window(padded, offset_x, offset_y, offset_z, extents) for offset_z in range(3)],
                axis=0,
            )
            section = lax.dot_general(
                grad_rows, stacked, (((1,), (1,)), ((), ())), preferred_element_type=jnp.float32
            )
            blocks.append(jnp.transpose(section.reshape(outputs, 3, inputs), (1, 0, 2)))
    return jnp.concatenate(blocks, axis=0)


def pool_cells(hidden):
    channels, size_x, size_y, size_z = hidden.shape
    pair_table = (jnp.arange(size_z)[:, None] // 2 == jnp.arange(size_z // 2)[None, :]).astype(
        jnp.bfloat16
    )
    depth_sums = jnp.dot(hidden.reshape(-1, size_z), pair_table, preferred_element_type=jnp.float32)
    depth_sums = depth_sums.reshape(channels, size_x // 2, 2, size_y // 2, 2, size_z // 2)
    return (0.125 * depth_sums.sum(axis=(2, 4))).astype(jnp.bfloat16)


def spread_cells(grad_field):
    scaled = 0.125 * grad_field
    scaled = jnp.repeat(scaled, 2, axis=1)
    scaled = jnp.repeat(scaled, 2, axis=2)
    return jnp.repeat(scaled, 2, axis=3)


def local(volume, first_weight, second_weight, cotangent):
    count_space = lax.axis_size("space")
    count_filt = lax.axis_size("filt")
    channels = volume.shape[0]
    fine_shape = volume.shape[1:]
    fine_cells = fine_shape[0] * fine_shape[1] * fine_shape[2] * count_space * count_filt
    fine_scale = 1.0 / fine_cells**0.5
    padded_in = pad_depth(extended(volume, (("space", 1), ("filt", 2)), 1))
    first_pre = conv_forward(padded_in, first_weight, fine_shape)
    hidden = jax.nn.silu(first_pre).astype(jnp.bfloat16).reshape((channels,) + fine_shape)
    pooled = pool_cells(hidden)
    brick_shape = pooled.shape[1:]
    brick_cells = brick_shape[0] * brick_shape[1] * brick_shape[2]
    bottom_scale = 1.0 / (brick_cells * count_space * count_filt) ** 0.5
    filters = second_weight.shape[1]
    gathered = collect(pooled, "filt", 2)
    slab_shape = gathered.shape[1:]
    padded_pool = jnp.pad(extended(gathered, (("space", 1),), 1), ((0, 0), (0, 0), (1, 1), (1, 1)))
    second_pre = conv_forward(padded_pool, second_weight, slab_shape)
    features = jax.nn.silu(second_pre).astype(jnp.bfloat16).reshape((filters,) + slab_shape)
    down_grad = (
        cotangent.reshape(filters, -1).astype(jnp.float32) * silu_slope(second_pre)
    ).astype(jnp.bfloat16)
    second_grad = (
        total_of_pieces(
            conv_weights(down_grad, padded_pool, slab_shape).astype(jnp.bfloat16), "space"
        ).astype(jnp.float32)
        * bottom_scale
    )
    padded_down = jnp.pad(
        extended(down_grad.reshape((filters,) + slab_shape), (("space", 1),), 1),
        ((0, 0), (0, 0), (1, 1), (1, 1)),
    )
    section = conv_transpose(padded_down, second_weight, slab_shape)
    rounded = (
        lax.optimization_barrier(section.astype(jnp.bfloat16))
        .astype(jnp.float32)
        .reshape((channels,) + slab_shape)
    )
    pool_grad = sum_at_owner(rounded.astype(jnp.bfloat16), "filt", 2).reshape(channels, brick_cells)
    hidden_grad = spread_cells(pool_grad.reshape((channels,) + brick_shape))
    first_down = (hidden_grad.reshape(channels, -1) * silu_slope(first_pre)).astype(jnp.bfloat16)
    first_grad = (
        lax.psum(conv_weights(first_down, padded_in, fine_shape), ("space", "filt")) * fine_scale
    )
    padded_back = pad_depth(
        extended(first_down.reshape((channels,) + fine_shape), (("space", 1), ("filt", 2)), 1)
    )
    volume_grad = (
        conv_transpose(padded_back, first_weight, fine_shape)
        .astype(jnp.bfloat16)
        .reshape((channels,) + fine_shape)
    )
    return (features, volume_grad, first_grad, second_grad)


def solution(mesh):
    placed = (
        P(None, "space", "filt", None),
        P(),
        P(None, "filt", None),
        P("filt", "space", None, None),
    )
    return jax.shard_map(
        local,
        mesh=mesh,
        in_specs=placed,
        out_specs=(
            P("filt", "space", None, None),
            P(None, "space", "filt", None),
            P(),
            P(None, "filt", None),
        ),
        check_vma=False,
    )
```

profile of v0, /device:TPU:1, one launch (start us, length us, event | category | flops | bytes accessed | tf_op | source)
XLA Modules:
  0.0 413.5 jit_solution(10433942499611277230)
XLA Ops:
  8.0 1.0 fusion.146
  9.0 6.3 %collective-permute-start = (bf16[64,1,2,256]{3,2,1,0:T(2,128)(2,1)S(1)}, bf16[64,1,2,256]{3,2,1,0:T(2,128)(2,1)S(1)}, u32[]{:S(2)}, u32[]{:S(2)}) collective-permute-start(bf16[64,1,2,256]{3,2,1,0:T(2,128)(2,1)S(1)} %get-tuple-element.151), channel_id=1, source_target_pairs={{0,8},{8,16},{16,24},{24,32},{32,40},{40,48},{48,56},{56,64},{64,7... | collective-permute-start | bytes 196616 | tf_op jit(solution)/shard_map/ppermute | solution.py:15
  15.3 1.9 collective-permute-start.1
  17.3 4.5 %collective-permute-done.1 = bf16[64,1,2,256]{3,2,1,0:T(2,128)(2,1)S(1)} collective-permute-done((bf16[64,1,2,256]{3,2,1,0:T(2,128)(2,1)S(1)}, bf16[64,1,2,256]{3,2,1,0:T(2,128)(2,1)S(1)}, u32[]{:S(2)}, u32[]{:S(2)}) %collective-permute-start.1) | collective-permute-done | bytes 65568 | tf_op jit(solution)/shard_map/ppermute | solution.py:17
  21.8 1.3 pad_maximum_fusion.9
  23.6 3.1 collective-permute-start.2
  26.7 1.3 collective-permute-start.3
  37.5 2.4 select_maximum_fusion.4
  39.9 3.6 fusion.138
  43.6 2.5 pad_maximum_fusion.8
  52.5 1.6 reshape.800
  60.4 1.6 reshape.812
  62.0 1.6 reshape.813
  63.7 1.0 constant_dynamic-update-slice_fusion.4
  65.6 1.1 fusion.148
  72.6 6.2 %all-to-all-start = ((bf16[8,64,1,1,128]{4,1,3,2,0:T(8,128)(2,1)}), bf16[8,64,1,1,128]{4,1,3,2,0:T(8,128)(2,1)S(1)}, u32[]{:S(2)}, u32[]{:S(2)}) async-start(bf16[8,64,1,1,128]{4,1,3,2,0:T(8,128)(2,1)} %broadcast_in_dim.4), calls=%async_computation | async-start | bytes 262144 | tf_op jit(solution)/shard_map/all_to_all | solution.py:26
  79.9 4.4 %all-to-all-done = bf16[8,64,1,1,128]{4,1,3,2,0:T(8,128)(2,1)S(1)} async-done(((bf16[8,64,1,1,128]{4,1,3,2,0:T(8,128)(2,1)}), bf16[8,64,1,1,128]{4,1,3,2,0:T(8,128)(2,1)S(1)}, u32[]{:S(2)}, u32[]{:S(2)}) %all-to-all-start) | async-done | bytes 131104 | tf_op jit(solution)/shard_map/all_to_all | solution.py:26
  84.4 3.9 collective-permute-start.4
  88.3 2.1 collective-permute-start.5
  90.4 7.0 %collective-permute-done.5 = bf16[64,1,8,128]{3,2,0,1:T(8,128)(2,1)S(1)} collective-permute-done((bf16[64,1,8,128]{3,2,0,1:T(8,128)(2,1)S(1)}, bf16[64,1,8,128]{3,2,0,1:T(8,128)(2,1)S(1)}, u32[]{:S(2)}, u32[]{:S(2)}) %collective-permute-start.5) | collective-permute-done | bytes 131104 | tf_op jit(solution)/shard_map/ppermute | solution.py:17
  97.4 1.1 select_maximum_fusion
  103.8 1.9 collective-permute-start.6
  105.7 2.4 collective-permute-start.7
  108.9 6.1 %collective-permute-done.7 = bf16[16,1,8,128]{3,2,0,1:T(8,128)(2,1)S(1)} collective-permute-done((bf16[16,1,8,128]{3,2,0,1:T(8,128)(2,1)S(1)}, bf16[16,1,8,128]{3,2,0,1:T(8,128)(2,1)S(1)}, u32[]{:S(2)}, u32[]{:S(2)}) %collective-permute-start.7) | collective-permute-done | bytes 32800 | tf_op jit(solution)/shard_map/ppermute | solution.py:17
  118.7 3.4 all-to-all-start.1
  122.2 1.8 convolution_convert_fusion.7
  124.0 3.5 all-to-all-done.1
  128.6 1.9 copy.73
  130.5 1.1 multiply_convert_fusion
  131.6 1.2 fusion.157
  137.8 3.1 collective-permute-start.8
  143.1 1.9 collective-permute-start.9
  145.1 5.6 %collective-permute-done.9 = bf16[64,1,2,256]{3,2,1,0:T(2,128)(2,1)S(1)} collective-permute-done((bf16[64,1,2,256]{3,2,1,0:T(2,128)(2,1)S(1)}, bf16[64,1,2,256]{3,2,1,0:T(2,128)(2,1)S(1)}, u32[]{:S(2)}, u32[]{:S(2)}) %collective-permute-start.9) | collective-permute-done | bytes 65568 | tf_op jit(solution)/shard_map/ppermute | solution.py:17
  151.5 2.4 collective-permute-start.10
  153.9 1.5 collective-permute-start.11
  161.9 1.7 pad_maximum_fusion
  164.3 2.4 select_maximum_fusion.2
  166.8 3.6 fusion.137
  170.4 1.0 reshape.891
  171.3 1.6 reshape.893
  174.0 1.6 reshape.897
  178.4 1.2 fusion.19
  179.6 1.0 convolution_add_fusion.7
  180.7 1.0 convolution_add_fusion.6
  184.2 215.8 %all-reduce.6.cloned.1.call-done = f32[27,64,64]{1,2,0:T(8,128)} async-done(((f32[27,64,64]{1,2,0:T(8,128)}), f32[27,64,64]{1,2,0:T(8,128)}) %all-reduce.6.cloned.1.call-update) | async-done | bytes 442384 | tf_op jit(solution)/shard_map/psum | solution.py:184
  400.0 1.3 broadcast_multiply_fusion
  401.3 1.2 copy.86
  402.5 2.7 convert_reduce_fusion
  (403 shorter events, 62.2 us)
Async XLA Ops:
  8.0 20.0 %copy-start.28 = (bf16[27,64,64]{2,1,0:T(8,128)(2,1)S(1)}, bf16[27,64,64]{2,1,0:T(8,128)(2,1)}, u32[]{:S(2)}) copy-start(bf16[27,64,64]{2,1,0:T(8,128)(2,1)} %param.5) | copy-start | bytes 663556
  9.0 8.2 %collective-permute-start = (bf16[64,1,2,256]{3,2,1,0:T(2,128)(2,1)S(1)}, bf16[64,1,2,256]{3,2,1,0:T(2,128)(2,1)S(1)}, u32[]{:S(2)}, u32[]{:S(2)}) collective-permute-start(bf16[64,1,2,256]{3,2,1,0:T(2,128)(2,1)S(1)} %get-tuple-element.151), channel_id=1, source_target_pairs={{0,8},{8,16},{16,24},{24,32},{32,40},{40,48},{48,56},{56,64},{64,7... | collective-permute-start | bytes 196616 | tf_op jit(solution)/shard_map/ppermute | solution.py:15
  15.3 6.5 %collective-permute-start.1 = (bf16[64,1,2,256]{3,2,1,0:T(2,128)(2,1)S(1)}, bf16[64,1,2,256]{3,2,1,0:T(2,128)(2,1)S(1)}, u32[]{:S(2)}, u32[]{:S(2)}) collective-permute-start(bf16[64,1,2,256]{3,2,1,0:T(2,128)(2,1)S(1)} %get-tuple-element.150), channel_id=1, source_target_pairs={{8,0},{16,8},{24,16},{32,24},{40,32},{48,40},{56,48},{64,56},{72,6... | collective-permute-start | bytes 196616 | tf_op jit(solution)/shard_map/ppermute | solution.py:17
  17.3 11.6 %copy-start.3 = (bf16[64,2,2,256]{3,2,1,0:T(2,128)(2,1)S(1)}, bf16[64,2,2,256]{3,2,1,0:T(2,128)(2,1)}, u32[]{:S(2)}) copy-start(bf16[64,2,2,256]{3,2,1,0:T(2,128)(2,1)} %param.4) | copy-start | bytes 393220
  23.6 13.9 %collective-permute-start.2 = (bf16[64,4,1,256]{3,2,1,0:T(2,128)(2,1)S(1)}, bf16[64,4,1,256]{3,2,1,0:T(2,128)(2,1)S(1)}, u32[]{:S(2)}, u32[]{:S(2)}) collective-permute-start(bf16[64,4,1,256]{3,2,1,0:T(2,128)(2,1)S(1)} %get-tuple-element.138), channel_id=1, source_target_pairs={{0,1},{1,2},{2,3},{3,4},{4,5},{5,6},{6,7},{8,9},{9,10},{10,11},{11... | collective-permute-start | bytes 393224 | tf_op jit(solution)/shard_map/ppermute | solution.py:15
  26.7 10.8 %collective-permute-start.3 = (bf16[64,4,1,256]{3,2,1,0:T(2,128)(2,1)S(1)}, bf16[64,4,1,256]{3,2,1,0:T(2,128)(2,1)S(1)}, u32[]{:S(2)}, u32[]{:S(2)}) collective-permute-start(bf16[64,4,1,256]{3,2,1,0:T(2,128)(2,1)S(1)} %get-tuple-element.139), channel_id=1, source_target_pairs={{1,0},{2,1},{3,2},{4,3},{5,4},{6,5},{7,6},{9,8},{10,9},{11,10},{12... | collective-permute-start | bytes 393224 | tf_op jit(solution)/shard_map/ppermute | solution.py:17
  43.5 3.4 copy-start.10
  43.5 4.1 copy-start.9
  43.5 4.2 %copy-start.8 = (bf16[64,2,2,256]{3,2,1,0:T(2,128)(2,1)S(1)}, bf16[64,2,2,256]{3,2,1,0:T(2,128)(2,1)}, u32[]{:S(2)}) copy-start(bf16[64,2,2,256]{3,2,1,0:T(2,128)(2,1)} %get-tuple-element.72) | copy-start | bytes 393220
  43.6 4.8 %copy-start.7 = (bf16[64,2,2,256]{3,2,1,0:T(2,128)(2,1)S(1)}, bf16[64,2,2,256]{3,2,1,0:T(2,128)(2,1)}, u32[]{:S(2)}) copy-start(bf16[64,2,2,256]{3,2,1,0:T(2,128)(2,1)} %get-tuple-element.71) | copy-start | bytes 393220
  43.6 5.7 %copy-start.6 = (bf16[64,2,2,256]{3,2,1,0:T(2,128)(2,1)S(1)}, bf16[64,2,2,256]{3,2,1,0:T(2,128)(2,1)}, u32[]{:S(2)}) copy-start(bf16[64,2,2,256]{3,2,1,0:T(2,128)(2,1)} %get-tuple-element.70) | copy-start | bytes 393220
  46.2 3.9 copy-start.11
  63.6 4.1 copy-start.15
  63.6 4.1 copy-start.16
  63.6 4.1 %copy-start.17 = (bf16[64,1024]{1,0:T(8,128)(2,1)S(1)}, bf16[64,1024]{1,0:T(8,128)(2,1)}, u32[]{:S(2)}) copy-start(bf16[64,1024]{1,0:T(8,128)(2,1)} %reshape.789) | copy-start | bytes 393220
  63.6 4.2 %copy-start.18 = (bf16[64,1024]{1,0:T(8,128)(2,1)S(1)}, bf16[64,1024]{1,0:T(8,128)(2,1)}, u32[]{:S(2)}) copy-start(bf16[64,1024]{1,0:T(8,128)(2,1)} %reshape.792) | copy-start | bytes 393220
  63.6 4.2 %copy-start.19 = (bf16[64,1024]{1,0:T(8,128)(2,1)S(1)}, bf16[64,1024]{1,0:T(8,128)(2,1)}, u32[]{:S(2)}) copy-start(bf16[64,1024]{1,0:T(8,128)(2,1)} %reshape.793) | copy-start | bytes 393220
  63.6 4.2 %copy-start.13 = (bf16[64,1024]{1,0:T(8,128)(2,1)S(1)}, bf16[64,1024]{1,0:T(8,128)(2,1)}, u32[]{:S(2)}) copy-start(bf16[64,1024]{1,0:T(8,128)(2,1)} %reshape.796) | copy-start | bytes 393220
  63.6 4.3 %copy-start.20 = (bf16[64,1024]{1,0:T(8,128)(2,1)S(1)}, bf16[64,1024]{1,0:T(8,128)(2,1)}, u32[]{:S(2)}) copy-start(bf16[64,1024]{1,0:T(8,128)(2,1)} %reshape.797) | copy-start | bytes 393220
  64.7 3.3 copy-start.21
  70.6 8.2 %copy-start.53 = (bf16[27,16,64]{2,1,0:T(8,128)(2,1)S(1)}, bf16[27,16,64]{2,1,0:T(8,128)(2,1)}, u32[]{:S(2)}) copy-start(bf16[27,16,64]{2,1,0:T(8,128)(2,1)} %param.6) | copy-start | bytes 165892
  71.6 18.8 %copy-start.59 = (bf16[16,1,8,128]{3,2,1,0:T(8,128)(2,1)S(1)}, bf16[16,1,8,128]{3,2,1,0:T(8,128)(2,1)}, u32[]{:S(2)}) copy-start(bf16[16,1,8,128]{3,2,1,0:T(8,128)(2,1)} %param.7) | copy-start | bytes 98308
  72.6 11.7 %all-to-all-start = ((bf16[8,64,1,1,128]{4,1,3,2,0:T(8,128)(2,1)}), bf16[8,64,1,1,128]{4,1,3,2,0:T(8,128)(2,1)S(1)}, u32[]{:S(2)}, u32[]{:S(2)}) async-start(bf16[8,64,1,1,128]{4,1,3,2,0:T(8,128)(2,1)} %broadcast_in_dim.4), calls=%async_computation | async-start | bytes 262144 | tf_op jit(solution)/shard_map/all_to_all | solution.py:26
  84.4 6.0 %collective-permute-start.4 = (bf16[64,1,8,128]{3,2,0,1:T(8,128)(2,1)S(1)}, bf16[64,1,8,128]{3,2,0,1:T(8,128)(2,1)S(1)}, u32[]{:S(2)}, u32[]{:S(2)}) collective-permute-start(bf16[64,1,8,128]{3,2,0,1:T(8,128)(2,1)S(1)} %bitcast.565), channel_id=1, source_target_pairs={{0,8},{8,16},{16,24},{24,32},{32,40},{40,48},{48,56},{56,64},{64,7... | collective-permute-start | bytes 393224 | tf_op jit(solution)/shard_map/ppermute | solution.py:15
  88.3 9.2 %collective-permute-start.5 = (bf16[64,1,8,128]{3,2,0,1:T(8,128)(2,1)S(1)}, bf16[64,1,8,128]{3,2,0,1:T(8,128)(2,1)S(1)}, u32[]{:S(2)}, u32[]{:S(2)}) collective-permute-start(bf16[64,1,8,128]{3,2,0,1:T(8,128)(2,1)S(1)} %bitcast.566), channel_id=1, source_target_pairs={{8,0},{16,8},{24,16},{32,24},{40,32},{48,40},{56,48},{64,56},{72,6... | collective-permute-start | bytes 393224 | tf_op jit(solution)/shard_map/ppermute | solution.py:17
  103.8 5.2 %collective-permute-start.6 = (bf16[16,1,8,128]{3,2,0,1:T(8,128)(2,1)S(1)}, bf16[16,1,8,128]{3,2,0,1:T(8,128)(2,1)S(1)}, u32[]{:S(2)}, u32[]{:S(2)}) collective-permute-start(bf16[16,1,8,128]{3,2,0,1:T(8,128)(2,1)S(1)} %bitcast.646), channel_id=1, source_target_pairs={{0,8},{8,16},{16,24},{24,32},{32,40},{40,48},{48,56},{56,64},{64,7... | collective-permute-start | bytes 98312 | tf_op jit(solution)/shard_map/ppermute | solution.py:15
  105.7 9.4 %collective-permute-start.7 = (bf16[16,1,8,128]{3,2,0,1:T(8,128)(2,1)S(1)}, bf16[16,1,8,128]{3,2,0,1:T(8,128)(2,1)S(1)}, u32[]{:S(2)}, u32[]{:S(2)}) collective-permute-start(bf16[16,1,8,128]{3,2,0,1:T(8,128)(2,1)S(1)} %bitcast.647), channel_id=1, source_target_pairs={{8,0},{16,8},{24,16},{32,24},{40,32},{48,40},{56,48},{64,56},{72,6... | collective-permute-start | bytes 98312 | tf_op jit(solution)/shard_map/ppermute | solution.py:17
  118.7 8.7 %all-to-all-start.1 = ((bf16[8,64,1,1,128]{4,1,3,2,0:T(8,128)(2,1)}), bf16[8,64,1,1,128]{4,1,3,2,0:T(8,128)(2,1)S(1)}, u32[]{:S(2)}, u32[]{:S(2)}) async-start(bf16[8,64,1,1,128]{4,1,3,2,0:T(8,128)(2,1)} %bitcast.553), calls=%async_computation.1 | async-start | bytes 262144 | tf_op jit(solution)/shard_map/all_to_all | solution.py:52
  122.1 277.9 %all-reduce.6.cloned.1.call-start = ((), (), s32[]{:S(2)}) async-start(), calls=%async_computation.2 | async-start | bytes 1769472 | tf_op jit(solution)/shard_map/psum | solution.py:184
  136.6 5.0 %copy-start.60 = (bf16[16,192]{1,0:T(8,128)(2,1)S(1)}, bf16[16,192]{1,0:T(8,128)(2,1)}, u32[]{:S(2)}) copy-start(bf16[16,192]{1,0:T(8,128)(2,1)} %convolution_convert_fusion.6) | copy-start | bytes 18436
  136.6 5.1 %copy-start.61 = (bf16[16,192]{1,0:T(8,128)(2,1)S(1)}, bf16[16,192]{1,0:T(8,128)(2,1)}, u32[]{:S(2)}) copy-start(bf16[16,192]{1,0:T(8,128)(2,1)} %convolution_convert_fusion.7) | copy-start | bytes 18436
  137.7 264.8 %all-gather.2.cloned.1.call-start = ((), (), s32[]{:S(2)}) async-start(), calls=%async_computation.3 | async-start | bytes 3649536 | tf_op jit(solution)/shard_map/all_gather | solution.py:41
  137.8 17.6 %copy-start.39 = (bf16[3,64,64]{2,1,0:T(8,128)(2,1)S(1)}, bf16[3,64,64]{2,1,0:T(8,128)(2,1)}, u32[]{:S(2)}) copy-start(bf16[3,64,64]{2,1,0:T(8,128)(2,1)} %get-tuple-element.104) | copy-start | bytes 73732
  137.8 7.2 %collective-permute-start.8 = (bf16[64,1,2,256]{3,2,1,0:T(2,128)(2,1)S(1)}, bf16[64,1,2,256]{3,2,1,0:T(2,128)(2,1)S(1)}, u32[]{:S(2)}, u32[]{:S(2)}) collective-permute-start(bf16[64,1,2,256]{3,2,1,0:T(2,128)(2,1)S(1)} %get-tuple-element.144), channel_id=1, source_target_pairs={{0,8},{8,16},{16,24},{24,32},{32,40},{40,48},{48,56},{56,64},{64,7... | collective-permute-start | bytes 196616 | tf_op jit(solution)/shard_map/ppermute | solution.py:15
  141.1 14.9 %copy-start.38 = (bf16[3,64,64]{2,1,0:T(8,128)(2,1)S(1)}, bf16[3,64,64]{2,1,0:T(8,128)(2,1)}, u32[]{:S(2)}) copy-start(bf16[3,64,64]{2,1,0:T(8,128)(2,1)} %get-tuple-element.105) | copy-start | bytes 73732
  141.1 15.5 %copy-start.37 = (bf16[3,64,64]{2,1,0:T(8,128)(2,1)S(1)}, bf16[3,64,64]{2,1,0:T(8,128)(2,1)}, u32[]{:S(2)}) copy-start(bf16[3,64,64]{2,1,0:T(8,128)(2,1)} %get-tuple-element.98) | copy-start | bytes 73732
  141.1 16.2 %copy-start.36 = (bf16[3,64,64]{2,1,0:T(8,128)(2,1)S(1)}, bf16[3,64,64]{2,1,0:T(8,128)(2,1)}, u32[]{:S(2)}) copy-start(bf16[3,64,64]{2,1,0:T(8,128)(2,1)} %get-tuple-element.99) | copy-start | bytes 73732
  141.5 16.4 %copy-start.35 = (bf16[3,64,64]{2,1,0:T(8,128)(2,1)S(1)}, bf16[3,64,64]{2,1,0:T(8,128)(2,1)}, u32[]{:S(2)}) copy-start(bf16[3,64,64]{2,1,0:T(8,128)(2,1)} %get-tuple-element.100) | copy-start | bytes 73732
  141.8 16.7 %copy-start.34 = (bf16[3,64,64]{2,1,0:T(8,128)(2,1)S(1)}, bf16[3,64,64]{2,1,0:T(8,128)(2,1)}, u32[]{:S(2)}) copy-start(bf16[3,64,64]{2,1,0:T(8,128)(2,1)} %get-tuple-element.101) | copy-start | bytes 73732
  141.9 17.3 %copy-start.33 = (bf16[3,64,64]{2,1,0:T(8,128)(2,1)S(1)}, bf16[3,64,64]{2,1,0:T(8,128)(2,1)}, u32[]{:S(2)}) copy-start(bf16[3,64,64]{2,1,0:T(8,128)(2,1)} %get-tuple-element.102) | copy-start | bytes 73732
  142.4 17.4 %copy-start.32 = (bf16[3,64,64]{2,1,0:T(8,128)(2,1)S(1)}, bf16[3,64,64]{2,1,0:T(8,128)(2,1)}, u32[]{:S(2)}) copy-start(bf16[3,64,64]{2,1,0:T(8,128)(2,1)} %get-tuple-element.103) | copy-start | bytes 73732
  142.4 17.4 %copy-start.31 = (bf16[3,64,64]{2,1,0:T(8,128)(2,1)S(1)}, bf16[3,64,64]{2,1,0:T(8,128)(2,1)}, u32[]{:S(2)}) copy-start(bf16[3,64,64]{2,1,0:T(8,128)(2,1)} %get-tuple-element.88) | copy-start | bytes 73732
  142.4 17.4 %copy-start.62 = (bf16[2,8,8,128]{3,1,2,0:T(8,128)(2,1)S(1)}, bf16[2,8,8,128]{3,1,2,0:T(8,128)(2,1)}, u32[]{:S(2)}) copy-start(bf16[2,8,8,128]{3,1,2,0:T(8,128)(2,1)} %get-tuple-element.171) | copy-start | bytes 98308
  143.1 7.6 %collective-permute-start.9 = (bf16[64,1,2,256]{3,2,1,0:T(2,128)(2,1)S(1)}, bf16[64,1,2,256]{3,2,1,0:T(2,128)(2,1)S(1)}, u32[]{:S(2)}, u32[]{:S(2)}) collective-permute-start(bf16[64,1,2,256]{3,2,1,0:T(2,128)(2,1)S(1)} %get-tuple-element.143), channel_id=1, source_target_pairs={{8,0},{16,8},{24,16},{32,24},{40,32},{48,40},{56,48},{64,56},{72,6... | collective-permute-start | bytes 196616 | tf_op jit(solution)/shard_map/ppermute | solution.py:17
  151.5 10.4 %collective-permute-start.10 = (bf16[64,4,1,256]{3,2,1,0:T(2,128)(2,1)S(1)}, bf16[64,4,1,256]{3,2,1,0:T(2,128)(2,1)S(1)}, u32[]{:S(2)}, u32[]{:S(2)}) collective-permute-start(bf16[64,4,1,256]{3,2,1,0:T(2,128)(2,1)S(1)} %get-tuple-element.133), channel_id=1, source_target_pairs={{0,1},{1,2},{2,3},{3,4},{4,5},{5,6},{6,7},{8,9},{9,10},{10,11},{11... | collective-permute-start | bytes 393224 | tf_op jit(solution)/shard_map/ppermute | solution.py:15
  153.9 8.0 %collective-permute-start.11 = (bf16[64,4,1,256]{3,2,1,0:T(2,128)(2,1)S(1)}, bf16[64,4,1,256]{3,2,1,0:T(2,128)(2,1)S(1)}, u32[]{:S(2)}, u32[]{:S(2)}) collective-permute-start(bf16[64,4,1,256]{3,2,1,0:T(2,128)(2,1)S(1)} %get-tuple-element.134), channel_id=1, source_target_pairs={{1,0},{2,1},{3,2},{4,3},{5,4},{6,5},{7,6},{9,8},{10,9},{11,10},{12... | collective-permute-start | bytes 393224 | tf_op jit(solution)/shard_map/ppermute | solution.py:17
  178.4 3.4 copy-start.52
  178.4 3.4 copy-start.58
  (31 other events, 43.1 us)
Sparse Core Ops, SparseCore 0:
  137.8 262.1 all-reduce.5
Sparse Core Ops, SparseCore 1:
  143.2 56.3 all-gather.1
where the time goes:
time: 415 us; the launch traced here: 414 us
  waiting for transfers between devices  247 us (60%)
  local copies, waits for them, and re-layouts  68.8 us (17%)
  starting transfers between devices  41.5 us (10%)
  matrix products  21.4 us (5%)
  between operations  17.6 us (4%)
  other arithmetic  17.3 us (4%)
    psum x1, waiting for transfers between devices, local(): lax.psum(conv_weights(first_down, padded_in, fine_shape), ('space', 'filt'))  216 us
    reshape x62, local copies, waits for them, and re-layouts, window(): return section.reshape(padded.shape[0], extent_x * extent_y * extent_z)  27.9 us
    ppermute x6, waiting for transfers between devices, extended(): lax.ppermute(head, axis, [((i + 1) % count, i) for i in range(ends)])  23.2 us
    ppermute x6, starting transfers between devices, extended(): lax.ppermute(tail, axis, [(i, (i + 1) % count) for i in range(ends)])  20.6 us
    concatenate x8, other arithmetic, extended(): jnp.concatenate([lax.ppermute(tail, axis, [(i, (i + 1) % count) for i in...  12.1 us
    ppermute x6, starting transfers between devices, extended(): lax.ppermute(head, axis, [((i + 1) % count, i) for i in range(ends)])  11.2 us
    unnamed x185, local copies, waits for them, and re-layouts  9.47 us
    dot_general x18, matrix products, conv_weights(): lax.dot_general(grad_rows, stacked, (((1,), (1,)), ((), ())), preferred_e...  8.63 us
  transfers between devices with their start and end apart: 16, of which 7 were waited for; matrix products, arithmetic and copies ran while one was open for 11% of the time, Pallas kernels for 0%

commit v1 on v0

v1 whole, which is shorter than its diff:
```python
import functools

import jax
import jax.numpy as jnp
from jax import lax
from jax.experimental import pallas as pl
from jax.experimental.pallas import tpu as pltpu
from jax.sharding import PartitionSpec as P

MESH = pl.DeviceIdType.MESH
F32 = jnp.float32
BF16 = jnp.bfloat16
DIRS = [(dx, dy) for dx in (-1, 0, 1) for dy in (-1, 0, 1) if (dx, dy) != (0, 0)]
N_SEMS = 128


def sigmoid(v):
    return 1.0 / (1.0 + jnp.exp(-v))


def shifted(values, by):
    if by == 0:
        return values
    length = values.shape[1]
    lane = lax.broadcasted_iota(jnp.int32, values.shape, 1)
    if by == 1:
        return jnp.where(lane == length - 1, 0.0, pltpu.roll(values, length - 1, 1))
    return jnp.where(lane == 0, 0.0, pltpu.roll(values, 1, 1))


def nt_dot(a, b):
    return lax.dot_general(a, b, (((1,), (1,)), ((), ())), preferred_element_type=F32)


def kernel(
    sizes,
    vol,
    cot,
    w1f,
    w1b,
    w2l,
    feat_out,
    vgrad_out,
    g1_out,
    g2_out,
    ext,
    fd,
    extd,
    slope1,
    cotg,
    w2g,
    w2b,
    ps,
    ds,
    featb,
    s_gb,
    s_cb,
    s_pb,
    s_fb,
    s_yr,
    s_zr,
    s_os,
    f_gb,
    f_cb,
    f_pb,
    f_fb,
    f_yr,
    f_zr,
    f_ag,
    send_sem,
    recv_sem,
):
    n_s, n_f, n_y, n_z = sizes
    s = lax.axis_index("space")
    f = lax.axis_index("filt")
    core = lax.rem(s, 2)
    zh = lax.rem(s // 2, n_z)
    y = s // (2 * n_z)
    fine_scale = 1.0 / float(n_s * 2 * n_f * 2 * 256) ** 0.5
    bottom_scale = 1.0 / float(n_s * n_f * 128) ** 0.5

    def near(dx, dy):
        return (lax.rem(s + dx + n_s, n_s), lax.rem(f + dy + n_f, n_f))

    def along_f(j):
        return (s, lax.rem(f + j, n_f))

    def along_y(j):
        return ((lax.rem(y + j, n_y) * n_z + zh) * 2 + core, f)

    def along_z(j):
        return ((y * n_z + lax.rem(zh + j, n_z)) * 2 + core, f)

    twin = (s + 1 - 2 * core, f)

    peers = [near(dx, dy) for dx, dy in DIRS]
    peers += [along_f(j) for j in range(1, n_f)]
    peers += [along_y(j) for j in range(1, n_y)]
    peers += [along_z(j) for j in range(1, n_z)]
    peers += [twin]
    barrier = pltpu.get_barrier_semaphore()
    for peer in peers:
        pl.semaphore_signal(barrier, inc=1, device_id=peer, device_id_type=MESH)
    pl.semaphore_wait(barrier, len(peers))

    sent = []

    def send(src, dst, device):
        at = len(sent)
        copy = pltpu.make_async_remote_copy(
            src_ref=src,
            dst_ref=dst,
            send_sem=send_sem.at[at],
            recv_sem=recv_sem.at[at],
            device_id=device,
            device_id_type=MESH,
        )
        copy.start()
        sent.append(copy)
        return at

    def arrive(ref, at):
        pltpu.make_async_copy(ref, ref, recv_sem.at[at]).wait()

    def src_part(d):
        return {1: 1, -1: 0, 0: slice(None)}[d]

    def dst_part(d):
        return {1: 0, -1: 3, 0: slice(1, 3)}[d]

    def halo_start(brick, field):
        out = []
        for dx, dy in DIRS:
            target = field.at[dst_part(dx), dst_part(dy)]
            out.append((send(brick.at[src_part(dx), src_part(dy)], target, near(dx, dy)), target))
        return out

    def finish(waits):
        for at, ref in waits:
            arrive(ref, at)

    def zero_rim(field, last):
        @pl.when(s == 0)
        def _():
            for b in range(last + 1):
                field[0, b] = jnp.zeros(field.shape[2:], field.dtype)

        @pl.when(s == n_s - 1)
        def _():
            for b in range(last + 1):
                field[last, b] = jnp.zeros(field.shape[2:], field.dtype)

        @pl.when(f == 0)
        def _():
            for a in range(last + 1):
                field[a, 0] = jnp.zeros(field.shape[2:], field.dtype)

        @pl.when(f == n_f - 1)
        def _():
            for a in range(last + 1):
                field[a, last] = jnp.zeros(field.shape[2:], field.dtype)

    vol_waits = halo_start(vol, ext)
    cot_waits = []
    w2_waits = []
    for j in range(1, n_f):
        other = lax.rem(f + j, n_f)
        source = lax.rem(f - j + n_f, n_f)
        cot_waits.append((send(cot.at[other], cotg.at[f], along_f(j)), cotg.at[source]))
    for j in range(1, n_f):
        source = lax.rem(f - j + n_f, n_f)
        w2_waits.append((send(w2l, w2g.at[f], along_f(j)), w2g.at[source]))
    for a in range(2):
        for b in range(2):
            ext[a + 1, b + 1] = vol[a, b]
    cotg[f] = cot[f]
    w2g[f] = w2l[...]
    ps[3, 0] = jnp.zeros((64, 128), BF16)
    pair_row = lax.broadcasted_iota(jnp.int32, (256, 128), 0)
    pair_col = lax.broadcasted_iota(jnp.int32, (256, 128), 1)
    below = pair_row - 2 * pair_col
    pairs = jnp.where((below == 0) | (below == 1), 1.0, 0.0).astype(BF16)

    def stack(field, a, b):
        planes = [field[a + i, b + j] for i in range(3) for j in range(3)]
        return jnp.concatenate(planes + [jnp.zeros((64, 256), BF16)], axis=0)

    finish(vol_waits)
    zero_rim(ext, 3)

    wf = w1f[...]
    total = jnp.zeros((64, 128), F32)
    for a in range(2):
        for b in range(2):
            rows = jnp.dot(wf, stack(ext, a, b), preferred_element_type=F32)
            pre = shifted(rows[0:64], -1) + rows[64:128] + shifted(rows[128:192], 1)
            gate = sigmoid(pre)
            slope1[a, b] = gate * (1.0 + pre * (1.0 - gate))
            hidden = (pre * gate).astype(BF16)
            total = total + jnp.dot(hidden, pairs, preferred_element_type=F32)
    ps[1, 1] = (0.125 * total).astype(BF16)

    pool_waits = []
    for dx, dy in DIRS:
        target = ps.at[1 - dx, 1 - dy]
        pool_waits.append((send(ps.at[1, 1], target, near(dx, dy)), target))

    finish(cot_waits)
    finish(w2_waits)
    w2 = w2g[...].reshape(n_f * 48, 640)
    for dz in range(3):
        block = w2g[:, 16 * dz : 16 * dz + 16, :].reshape(128, 640).astype(F32)
        turned = block.T.astype(BF16)
        for slot in range(9):
            w2b[64 * dz : 64 * dz + 64, 128 * (8 - slot) : 128 * (8 - slot) + 128] = turned[
                64 * slot : 64 * slot + 64
            ]

    finish(pool_waits)
    zero_rim(ps, 2)

    around = jnp.concatenate(
        [ps[i, j] for i in range(3) for j in range(3)] + [ps[3, 0]], axis=0
    )
    rows = jnp.dot(w2, around, preferred_element_type=F32).reshape(n_f, 3, 16, 128)
    pre = (
        shifted(rows[:, 0].reshape(128, 128), -1)
        + rows[:, 1].reshape(128, 128)
        + shifted(rows[:, 2].reshape(128, 128), 1)
    )
    gate = sigmoid(pre)
    down = cotg[...].reshape(128, 128).astype(F32) * (gate * (1.0 + pre * (1.0 - gate)))
    ds[1, 1] = down.astype(BF16)
    featb[0] = (pre * gate).astype(BF16).reshape(n_f, 16, 128)

    down_waits = []
    for dx, dy in DIRS:
        target = ds.at[1 - dx, 1 - dy]
        down_waits.append((send(ds.at[1, 1], target, near(dx, dy)), target))
    feat_waits = []
    for j in range(1, n_f):
        other = lax.rem(f + j, n_f)
        source = lax.rem(f - j + n_f, n_f)
        feat_waits.append(
            (send(featb.at[0, other], featb.at[1, f], along_f(j)), featb.at[1, source])
        )
    featb[1, f] = featb[0, f]

    moved = [shifted(down, 1).astype(BF16), down.astype(BF16), shifted(down, -1).astype(BF16)]
    lhs = jnp.concatenate(
        [moved[dz][16 * g : 16 * g + 16] for g in range(n_f) for dz in range(3)], axis=0
    )
    terms = nt_dot(lhs, around)

    def deal(values, height, buffer):
        per = values.shape[0] // n_f
        for g in range(n_f):
            tiles = [
                values[per * g + height * r : per * g + height * r + height, 128 * c : 128 * c + 128]
                for r in range(3)
                for c in range(5)
            ]
            tiles.append(jnp.zeros((height, 128), F32))
            for half in range(2):
                piece = jnp.concatenate(tiles[8 * half : 8 * half + 8], axis=0)
                buffer[half, g] = piece.astype(BF16)

    deal(terms, 16, s_gb)

    def to_twin(gb, cb):
        return [(send(gb.at[1 - core], cb, twin), cb)]

    def over_filt(gb, cb, pb, fb):
        pb[...] = (gb[core].astype(F32) + cb[...].astype(F32)).astype(BF16)
        fb[f] = pb[f]
        waits = []
        for j in range(1, n_f):
            other = lax.rem(f + j, n_f)
            source = lax.rem(f - j + n_f, n_f)
            waits.append((send(pb.at[other], fb.at[f], along_f(j)), fb.at[source]))
        return waits

    def summed(ref, count):
        value = ref[0].astype(F32)
        for k in range(1, count):
            value = value + ref[k].astype(F32)
        return value.astype(BF16)

    def over_y(fb, yr):
        yr[y] = summed(fb, n_f)
        waits = []
        for j in range(1, n_y):
            source = lax.rem(y - j + n_y, n_y)
            waits.append((send(yr.at[y], yr.at[y], along_y(j)), yr.at[source]))
        return waits

    def over_z(yr, zr):
        zr[zh] = summed(yr, n_y)
        waits = []
        for j in range(1, n_z):
            source = lax.rem(zh - j + n_z, n_z)
            waits.append((send(zr.at[zh], zr.at[zh], along_z(j)), zr.at[source]))
        return waits

    s_waits = to_twin(s_gb, s_cb)

    finish(down_waits)
    zero_rim(ds, 2)
    planes = jnp.concatenate([ds[i, j] for i in range(3) for j in range(3)], axis=0)
    rows = jnp.dot(w2b[...], planes, preferred_element_type=F32)
    pool_grad = 0.125 * (
        shifted(rows[0:64], 1) + rows[64:128] + shifted(rows[128:192], -1)
    )
    high = pool_grad.astype(BF16)
    low = (pool_grad - high.astype(F32)).astype(BF16)
    spread = nt_dot(jnp.concatenate([high, low], axis=0), pairs)
    spread = spread[0:64] + spread[64:128]
    for a in range(2):
        for b in range(2):
            fd[a, b] = (spread * slope1[a, b]).astype(BF16)
    fd_waits = halo_start(fd, extd)

    terms = jnp.zeros((192, 640), F32)
    for a in range(2):
        for b in range(2):
            own = fd[a, b]
            extd[a + 1, b + 1] = own
            wide = own.astype(F32)
            lhs = jnp.concatenate(
                [shifted(wide, 1).astype(BF16), own, shifted(wide, -1).astype(BF16)], axis=0
            )
            terms = terms + nt_dot(lhs, stack(ext, a, b))
    deal(terms, 8, f_gb)
    f_waits = to_twin(f_gb, f_cb)

    finish(s_waits)
    s_waits = over_filt(s_gb, s_cb, s_pb, s_fb)
    finish(f_waits)
    f_waits = over_filt(f_gb, f_cb, f_pb, f_fb)

    finish(fd_waits)
    zero_rim(extd, 3)
    wb = w1b[...]
    for a in range(2):
        for b in range(2):
            rows = jnp.dot(wb, stack(extd, a, b), preferred_element_type=F32)
            vgrad_out[a, b] = (
                shifted(rows[0:64], 1) + rows[64:128] + shifted(rows[128:192], -1)
            ).astype(BF16)
    finish(feat_waits)
    feat_out[...] = featb[1]

    finish(f_waits)
    f_waits = over_y(f_fb, f_yr)
    finish(s_waits)
    s_waits = over_y(s_fb, s_yr)
    finish(f_waits)
    f_waits = over_z(f_yr, f_zr)
    finish(s_waits)
    s_waits = over_z(s_yr, s_zr)
    finish(f_waits)
    f_ag[core, f] = summed(f_zr, n_z)
    f_waits = []
    for j in range(1, n_f):
        source = lax.rem(f - j + n_f, n_f)
        f_waits.append((send(f_ag.at[core, f], f_ag.at[core, f], along_f(j)), f_ag.at[core, source]))
    finish(s_waits)
    s_os[core] = summed(s_zr, n_z)
    s_waits = [(send(s_os.at[core], s_os.at[core], twin), s_os.at[1 - core])]
    finish(s_waits)

    def lay_out(read, height, scale, store):
        for k in range(15):
            tile = read(k) * scale
            dz, c = k // 5, k % 5
            store(6 * c + dz, tile[:, 0:64])
            if c < 4:
                store(6 * c + 3 + dz, pltpu.roll(tile, 64, 1)[:, 0:64])

    halves = [s_os[h].astype(F32) for h in range(2)]

    def store_bottom(tap, value):
        g2_out[tap] = value

    lay_out(
        lambda k: halves[k // 8][16 * (k % 8) : 16 * (k % 8) + 16], 16, bottom_scale, store_bottom
    )

    finish(f_waits)
    f_waits = [(send(f_ag.at[core], f_ag.at[core], twin), f_ag.at[1 - core])]
    finish(f_waits)
    for g in range(n_f):
        both = [f_ag[h, g].astype(F32) for h in range(2)]
        for k in range(15):
            row = 24 * g + 8 * (k // 5)
            dz, o = row // 64, row % 64
            c = k % 5
            tile = both[k // 8][8 * (k % 8) : 8 * (k % 8) + 8] * fine_scale
            g1_out[6 * c + dz, o : o + 8] = tile[:, 0:64]
            if c < 4:
                g1_out[6 * c + 3 + dz, o : o + 8] = pltpu.roll(tile, 64, 1)[:, 0:64]

    for copy in sent:
        copy.wait_send()


def local(sizes, volume, first_weight, second_weight, cotangent):
    n_s, n_f, n_y, n_z = sizes
    vol = jnp.transpose(volume, (1, 2, 0, 3))
    cot = jnp.transpose(cotangent[:, 0], (1, 0, 2))
    pad = ((0, 0), (0, 64))
    taps = first_weight.reshape(9, 3, 64, 64)
    w1f = jnp.pad(jnp.transpose(taps, (1, 2, 0, 3)).reshape(192, 576), pad)
    w1b = jnp.pad(jnp.transpose(taps[::-1], (1, 3, 0, 2)).reshape(192, 576), pad)
    bottom = second_weight.reshape(9, 3, 16, 64)
    w2l = jnp.pad(jnp.transpose(bottom, (1, 2, 0, 3)).reshape(48, 576), pad)
    vmem = pl.BlockSpec(memory_space=pltpu.VMEM)
    features, volume_grad, first_grad, second_grad = pl.pallas_call(
        functools.partial(kernel, sizes),
        out_shape=(
            jax.ShapeDtypeStruct((n_f, 16, 128), BF16),
            jax.ShapeDtypeStruct((2, 2, 64, 256), BF16),
            jax.ShapeDtypeStruct((27, 64, 64), F32),
            jax.ShapeDtypeStruct((27, 16, 64), F32),
        ),
        in_specs=[vmem] * 5,
        out_specs=(vmem,) * 4,
        scratch_shapes=[
            pltpu.VMEM((4, 4, 64, 256), BF16),
            pltpu.VMEM((2, 2, 64, 256), BF16),
            pltpu.VMEM((4, 4, 64, 256), BF16),
            pltpu.VMEM((2, 2, 64, 256), F32),
            pltpu.VMEM((n_f, 16, 128), BF16),
            pltpu.VMEM((n_f, 48, 640), BF16),
            pltpu.VMEM((192, 1152), BF16),
            pltpu.VMEM((4, 3, 64, 128), BF16),
            pltpu.VMEM((3, 3, 128, 128), BF16),
            pltpu.VMEM((2, n_f, 16, 128), BF16),
            pltpu.VMEM((2, n_f, 128, 128), BF16),
            pltpu.VMEM((n_f, 128, 128), BF16),
            pltpu.VMEM((n_f, 128, 128), BF16),
            pltpu.VMEM((n_f, 128, 128), BF16),
            pltpu.VMEM((n_y, 128, 128), BF16),
            pltpu.VMEM((n_z, 128, 128), BF16),
            pltpu.VMEM((2, 128, 128), BF16),
            pltpu.VMEM((2, n_f, 64, 128), BF16),
            pltpu.VMEM((n_f, 64, 128), BF16),
            pltpu.VMEM((n_f, 64, 128), BF16),
            pltpu.VMEM((n_f, 64, 128), BF16),
            pltpu.VMEM((n_y, 64, 128), BF16),
            pltpu.VMEM((n_z, 64, 128), BF16),
            pltpu.VMEM((2, n_f, 64, 128), BF16),
            pltpu.SemaphoreType.DMA((N_SEMS,)),
            pltpu.SemaphoreType.DMA((N_SEMS,)),
        ],
        compiler_params=pltpu.CompilerParams(collective_id=0, has_side_effects=True),
        name="block",
    )(vol, cot, w1f, w1b, w2l)
    return (
        jnp.transpose(features, (1, 0, 2))[:, None],
        jnp.transpose(volume_grad, (2, 0, 1, 3)),
        first_grad,
        second_grad,
    )


def solution(mesh):
    n_s, n_f = mesh.shape["space"], mesh.shape["filt"]
    n_z = 4 if n_s % 8 == 0 else 1
    sizes = (n_s, n_f, n_s // (2 * n_z), n_z)
    placed = (
        P(None, "space", "filt", None),
        P(),
        P(None, "filt", None),
        P("filt", "space", None, None),
    )
    return jax.shard_map(
        functools.partial(local, sizes),
        mesh=mesh,
        in_specs=placed,
        out_specs=(
            P("filt", "space", None, None),
            P(None, "space", "filt", None),
            P(),
            P(None, "filt", None),
        ),
        check_vma=False,
    )
```

time: 415 us -> 79.7 us (0.19)
  waiting for transfers between devices: 247 us -> 0 us
  Pallas kernels: 0 us -> 64.6 us
  local copies, waits for them, and re-layouts: 68.8 us -> 14.2 us
  starting transfers between devices: 41.5 us -> 0 us
  matrix products: 21.4 us -> 0 us
  other arithmetic: 17.3 us -> 0 us
  between operations: 17.6 us -> 0.68 us
    psum x1 -> x0, waiting for transfers between devices: 216 us -> none  [local(): lax.psum(conv_weights(first_down, padded_in, fine_shape), ('space', 'filt'))]
    pallas_call x0 -> x1, Pallas kernels: none -> 64.6 us  [local(): pl.pallas_call(functools.partial(kernel, sizes), out_shape=(jax.ShapeDtyp...]
    ppermute x12 -> x0, starting transfers between devices: 31.8 us -> none  [the longest x6 20.6 us: extended(): lax.ppermute(tail, axis, [(i, (i + 1) % count) for i in range(ends)])]
    reshape x82 -> x8, local copies, waits for them, and re-layouts: 30.2 us -> 2.88 us  [the longest x2 1.6 us: local(): taps = first_weight.reshape(9, 3, 64, 64)]
    ppermute x12 -> x0, waiting for transfers between devices: 23.2 us -> none  [the longest x6 23.2 us: extended(): lax.ppermute(head, axis, [((i + 1) % count, i) for i in range(ends)])]
    dot_general x55 -> x0, matrix products: 21.4 us -> none  [the longest x18 8.63 us: conv_weights(): lax.dot_general(grad_rows, stacked, (((1,), (1,)), ((), ())), preferred_e...]
    concatenate x8 -> x0, other arithmetic: 12.1 us -> none  [extended(): jnp.concatenate([lax.ppermute(tail, axis, [(i, (i + 1) % count) for i in...]
    slice x12 -> x0, local copies, waits for them, and re-layouts: 11.3 us -> none  [the longest x6 8.54 us: window(): lax.slice(padded, (0, offset_x, offset_y, offset_z), (padded.shape[0], of...]
  transfers between devices with their start and end apart: 16 -> 0, of which waited for: 7 -> 0; matrix products, arithmetic and copies ran while one was open for 11% -> 0% of each run, Pallas kernels for 0% -> 0%
where the time goes in v1:
time: 79.7 us; the launch traced here: 79.5 us
  Pallas kernels  64.6 us (81%)
  local copies, waits for them, and re-layouts  14.2 us (18%)
    pallas_call x1, Pallas kernels, local(): pl.pallas_call(functools.partial(kernel, sizes), out_shape=(jax.ShapeDtyp...  64.6 us
    unnamed x12, local copies, waits for them, and re-layouts  9.03 us
    reshape x2, local copies, waits for them, and re-layouts, local(): taps = first_weight.reshape(9, 3, 64, 64)  1.6 us

profile of v1, /device:TPU:1, one launch (start us, length us, event | category | flops | bytes accessed | tf_op | source)
XLA Modules:
  0.0 79.5 jit_solution(16429365832941547636)
XLA Ops:
  0.6 0.0 copy-start.2
  0.6 1.4 %copy.29 = bf16[16,1,8,128]{3,0,2,1:T(8,128)(2,1)} copy(bf16[16,1,8,128]{3,2,1,0:T(8,128)(2,1)} %param.7) | data formatting | bytes 65536 | tf_op args[3]
  2.1 0.0 copy-start
  2.1 1.6 %copy.28 = bf16[64,2,2,256]{3,0,2,1:T(8,128)(2,1)} copy(bf16[64,2,2,256]{3,2,1,0:T(2,128)(2,1)} %param.4) | data formatting | bytes 262144 | tf_op args[0]
  3.7 0.0 copy-done.2
  3.7 0.2 reshape.27
  3.9 0.6 pad.13.w2l
  4.5 0.0 copy-done
  4.5 0.4 copy.19
  4.9 0.2 reverse_bitcast_fusion
  5.2 0.4 reshape.25
  5.5 0.2 copy.20
  5.7 0.7 pad.12.w1b
  6.4 1.2 %copy.17 = bf16[9,3,64,64]{2,1,3,0:T(4,128)(2,1)S(1)} copy(bf16[9,3,64,64]{3,2,1,0:T(8,128)(2,1)S(1)} %bitcast.26) | data formatting | bytes 442368 | tf_op jit(solution)/shard_map/reshape | solution.py:412
  7.6 0.4 reshape.24
  8.0 0.2 copy.18
  8.2 0.7 pad.11.w1f
  8.9 64.6 %block.1 = (bf16[8,16,128]{2,1,0:T(8,128)(2,1)}, bf16[2,2,64,256]{3,2,1,0:T(8,128)(2,1)}, f32[27,64,64]{2,1,0:T(8,128)}, f32[27,16,64]{2,1,0:T(8,128)}) custom-call(bf16[2,2,64,256]{3,2,1,0:T(8,128)(2,1)} %bitcast.28, bf16[8,16,128]{2,1,0:T(8,128)(2,1)} %bitcast.29, bf16[192,640]{1,0:T(8,128)(2,1)} %pad.11.w1f, bf16[192,640]{1,0:T(8,128)(2,1)} %pad.12.w1b, ...), custom_call_target="tpu_custom_call" | custom-call | tf_op jit(solution)/shard_map/block/pallas_call | solution.py:418
  73.5 1.4 %copy.22 = bf16[16,1,8,128]{3,2,1,0:T(8,128)(2,1)} copy(bf16[16,1,8,128]{3,0,2,1:T(8,128)(2,1)} %bitcast.32) | data formatting | bytes 65536
  74.9 1.7 %copy.23 = bf16[64,2,2,256]{3,2,1,0:T(2,128)(2,1)} copy(bf16[64,2,2,256]{3,0,2,1:T(8,128)(2,1)} %bitcast.30) | data formatting | bytes 262144
  76.6 0.0 copy-start.1
  76.6 2.2 %copy.32 = f32[27,64,64]{2,1,0:T(8,128)} copy(f32[27,64,64]{2,1,0:T(8,128)} %get-tuple-element.26) | data formatting | bytes 884736
  78.8 0.0 copy-done.1
  78.8 0.7 copy.33
  (1 shorter events, 0.0 us)
Async XLA Ops:
  0.6 3.1 %copy-start.2 = (bf16[27,16,64]{2,1,0:T(8,128)(2,1)S(1)}, bf16[27,16,64]{2,1,0:T(8,128)(2,1)}, u32[]{:S(2)}) copy-start(bf16[27,16,64]{2,1,0:T(8,128)(2,1)} %param.6) | copy-start | bytes 165892
  2.1 2.5 %copy-start = (bf16[27,64,64]{2,1,0:T(8,128)(2,1)S(1)}, bf16[27,64,64]{2,1,0:T(8,128)(2,1)}, u32[]{:S(2)}) copy-start(bf16[27,64,64]{2,1,0:T(8,128)(2,1)} %param.5) | copy-start | bytes 663556
  76.6 2.2 %copy-start.1 = (f32[27,16,64]{2,1,0:T(8,128)S(1)}, f32[27,16,64]{2,1,0:T(8,128)}, u32[]{:S(2)}) copy-start(f32[27,16,64]{2,1,0:T(8,128)} %get-tuple-element.27) | copy-start | bytes 331780

commit v2 on v1

v2 whole, which is shorter than its diff:
```python
import functools

import jax
import jax.numpy as jnp
from jax import lax
from jax.experimental import pallas as pl
from jax.experimental.pallas import tpu as pltpu
from jax.sharding import PartitionSpec as P

MESH = pl.DeviceIdType.MESH
F32 = jnp.float32
BF16 = jnp.bfloat16
DIRS = [(dx, dy) for dx in (-1, 0, 1) for dy in (-1, 0, 1) if (dx, dy) != (0, 0)]
N_SEMS = 128


def sigmoid(v):
    return 1.0 / (1.0 + jnp.exp(-v))


def shifted(values, by):
    if by == 0:
        return values
    length = values.shape[1]
    lane = lax.broadcasted_iota(jnp.int32, values.shape, 1)
    if by == 1:
        return jnp.where(lane == length - 1, 0.0, pltpu.roll(values, length - 1, 1))
    return jnp.where(lane == 0, 0.0, pltpu.roll(values, 1, 1))


def nt_dot(a, b):
    return lax.dot_general(a, b, (((1,), (1,)), ((), ())), preferred_element_type=F32)


def side_by_side(left, right):
    return jnp.concatenate([left, right], axis=1)


def kernel(
    sizes,
    vol_hbm,
    cot_hbm,
    w1_hbm,
    w2_hbm,
    feat_out,
    vgrad_out,
    ag_out,
    os_out,
    vraw,
    craw,
    w1raw,
    w2raw,
    vrows,
    crows,
    cotb,
    w1f,
    w1b,
    w2p,
    ext,
    extd,
    slope1,
    cotg,
    w2g,
    w2t,
    ps,
    give,
    take,
    featb,
    s_gb,
    s_cb,
    s_pb,
    s_fb,
    s_yr,
    s_zr,
    s_os,
    f_gb,
    f_cb,
    f_pb,
    f_fb,
    f_yr,
    f_zr,
    f_ag,
    load_sem,
    send_sem,
    recv_sem,
):
    n_s, n_f, n_y, n_z = sizes
    s = lax.axis_index("space")
    f = lax.axis_index("filt")
    core = lax.rem(s, 2)
    zh = lax.rem(s // 2, n_z)
    y = s // (2 * n_z)

    loads = []
    for at, (whole, raw) in enumerate(
        ((vol_hbm, vraw), (w2_hbm, w2raw), (cot_hbm, craw), (w1_hbm, w1raw))
    ):
        load = pltpu.make_async_copy(whole, raw, load_sem.at[at])
        load.start()
        loads.append(load)

    def near(dx, dy):
        return (lax.rem(s + dx + n_s, n_s), lax.rem(f + dy + n_f, n_f))

    def along_f(j):
        return (s, lax.rem(f + j, n_f))

    def along_y(j):
        return ((lax.rem(y + j, n_y) * n_z + zh) * 2 + core, f)

    def along_z(j):
        return ((y * n_z + lax.rem(zh + j, n_z)) * 2 + core, f)

    twin = (s + 1 - 2 * core, f)

    peers = [near(dx, dy) for dx, dy in DIRS]
    peers += [along_f(j) for j in range(1, n_f)]
    peers += [along_y(j) for j in range(1, n_y)]
    peers += [along_z(j) for j in range(1, n_z)]
    peers += [twin]
    barrier = pltpu.get_barrier_semaphore()
    for peer in peers:
        pl.semaphore_signal(barrier, inc=1, device_id=peer, device_id_type=MESH)

    loads[0].wait()
    for c in range(64):
        for a in range(2):
            for h in range(2):
                vrows[h, 4 * c + 2 * a : 4 * c + 2 * a + 2] = vraw[
                    c, a, :, 128 * h : 128 * h + 128
                ].astype(F32)
    for a in range(2):
        for b in range(2):
            for h in range(2):
                ext[a + 1, b + 1, :, 128 * h : 128 * h + 128] = vrows[
                    h, pl.ds(2 * a + b, 64, stride=4), :
                ].astype(BF16)
    pl.semaphore_wait(barrier, len(peers))

    sent = []

    def send(src, dst, device):
        at = len(sent)
        copy = pltpu.make_async_remote_copy(
            src_ref=src,
            dst_ref=dst,
            send_sem=send_sem.at[at],
            recv_sem=recv_sem.at[at],
            device_id=device,
            device_id_type=MESH,
        )
        copy.start()
        sent.append(copy)
        return at

    def arrive(ref, at):
        pltpu.make_async_copy(ref, ref, recv_sem.at[at]).wait()

    def src_part(d):
        return {1: 2, -1: 1, 0: slice(1, 3)}[d]

    def dst_part(d):
        return {1: 0, -1: 3, 0: slice(1, 3)}[d]

    def halo_start(field):
        out = []
        for dx, dy in DIRS:
            target = field.at[dst_part(dx), dst_part(dy)]
            source = field.at[src_part(dx), src_part(dy)]
            out.append((send(source, target, near(dx, dy)), target))
        return out

    def finish(waits):
        for at, ref in waits:
            arrive(ref, at)

    def zero_rim(field, last):
        @pl.when(s == 0)
        def _():
            for b in range(last + 1):
                field[0, b] = jnp.zeros(field.shape[2:], field.dtype)

        @pl.when(s == n_s - 1)
        def _():
            for b in range(last + 1):
                field[last, b] = jnp.zeros(field.shape[2:], field.dtype)

        @pl.when(f == 0)
        def _():
            for a in range(last + 1):
                field[a, 0] = jnp.zeros(field.shape[2:], field.dtype)

        @pl.when(f == n_f - 1)
        def _():
            for a in range(last + 1):
                field[a, last] = jnp.zeros(field.shape[2:], field.dtype)

    vol_waits = halo_start(ext)

    loads[1].wait()
    for k in range(15):
        dz, c = k // 5, k % 5
        right = w2raw[6 * c + 3 + dz] if c < 4 else jnp.zeros((16, 64), BF16)
        w2p[k] = side_by_side(w2raw[6 * c + dz], right)
    w2p[15] = jnp.zeros((16, 128), BF16)
    half = w2p.at[pl.ds(8 * core, 8)]
    w2_waits = []
    for j in range(1, n_f):
        source = lax.rem(f - j + n_f, n_f)
        w2_waits.append((send(half, w2g.at[core, f], along_f(j)), w2g.at[core, source]))
    w2g[core, f] = w2p[pl.ds(8 * core, 8)]

    loads[2].wait()
    crows[...] = craw[...].reshape(16 * n_f, 128).astype(F32)
    for k in range(n_f):
        cotb[k] = crows[pl.ds(k, 16, stride=n_f), :].astype(BF16)
    cot_waits = []
    for j in range(1, n_f):
        other = lax.rem(f + j, n_f)
        source = lax.rem(f - j + n_f, n_f)
        cot_waits.append((send(cotb.at[other], cotg.at[f], along_f(j)), cotg.at[source]))
    cotg[f] = cotb[f]

    loads[3].wait()
    for k in range(15):
        dz, c = k // 5, k % 5
        rows = slice(64 * dz, 64 * dz + 64)
        cols = slice(128 * c, 128 * c + 128)
        right = w1raw[6 * c + 3 + dz] if c < 4 else jnp.zeros((64, 64), BF16)
        w1f[rows, cols] = side_by_side(w1raw[6 * c + dz], right)
        back = [w1raw[3 * (8 - 2 * c) + dz]]
        back.append(w1raw[3 * (7 - 2 * c) + dz] if c < 4 else jnp.zeros((64, 64), BF16))
        w1b[rows, cols] = jnp.concatenate(back, axis=0).astype(F32).T.astype(BF16)
    ps[3, 0] = jnp.zeros((64, 128), BF16)
    pair_row = lax.broadcasted_iota(jnp.int32, (256, 128), 0)
    pair_col = lax.broadcasted_iota(jnp.int32, (256, 128), 1)
    below = pair_row - 2 * pair_col
    pairs = jnp.where((below == 0) | (below == 1), 1.0, 0.0).astype(BF16)

    def stack(field, a, b):
        planes = [field[a + i, b + j] for i in range(3) for j in range(3)]
        return jnp.concatenate(planes + [jnp.zeros((64, 256), BF16)], axis=0)

    finish(vol_waits)
    zero_rim(ext, 3)

    wf = w1f[...]
    total = jnp.zeros((64, 128), F32)
    for a in range(2):
        for b in range(2):
            rows = jnp.dot(wf, stack(ext, a, b), preferred_element_type=F32)
            pre = shifted(rows[0:64], -1) + rows[64:128] + shifted(rows[128:192], 1)
            gate = sigmoid(pre)
            slope1[a, b] = gate * (1.0 + pre * (1.0 - gate))
            hidden = (pre * gate).astype(BF16)
            total = total + jnp.dot(hidden, pairs, preferred_element_type=F32)
    ps[1, 1] = (0.125 * total).astype(BF16)

    pool_waits = []
    for dx, dy in DIRS:
        target = ps.at[1 - dx, 1 - dy]
        pool_waits.append((send(ps.at[1, 1], target, near(dx, dy)), target))

    finish(w2_waits)
    w2_waits = [(send(w2g.at[core], w2g.at[core], twin), w2g.at[1 - core])]
    finish(cot_waits)
    finish(w2_waits)
    w2 = []
    for dz in range(3):
        tiles = [
            w2g[k // 8, :, k % 8].reshape(16 * n_f, 128) for k in range(5 * dz, 5 * dz + 5)
        ]
        w2.append(jnp.concatenate(tiles, axis=1))
        for c in range(5):
            w2t[dz, 128 * c : 128 * c + 128] = tiles[c].astype(F32).T.astype(BF16)

    finish(pool_waits)
    zero_rim(ps, 2)

    around = jnp.concatenate(
        [ps[i, j] for i in range(3) for j in range(3)] + [ps[3, 0]], axis=0
    )
    rows = [jnp.dot(w, around, preferred_element_type=F32) for w in w2]
    pre = shifted(rows[0], -1) + rows[1] + shifted(rows[2], 1)
    gate = sigmoid(pre)
    down = cotg[...].reshape(128, 128).astype(F32) * (gate * (1.0 + pre * (1.0 - gate)))
    down_own = down.astype(BF16)

    rows = [jnp.dot(w2t[dz], down_own, preferred_element_type=F32) for dz in range(3)]
    share = shifted(rows[0], 1) + rows[1] + shifted(rows[2], -1)
    down_waits = []
    for dx, dy in DIRS:
        slot = 3 * (dx + 1) + dy + 1
        give[slot] = share[64 * slot : 64 * slot + 64].astype(BF16)
        target = take.at[1 - dx, 1 - dy]
        down_waits.append((send(give.at[slot], target, near(dx, dy)), target))
    own_share = share[256:320]
    featb[0] = (pre * gate).astype(BF16).reshape(n_f, 16, 128)

    feat_waits = []
    for j in range(1, n_f):
        other = lax.rem(f + j, n_f)
        source = lax.rem(f - j + n_f, n_f)
        feat_waits.append(
            (send(featb.at[0, other], featb.at[1, f], along_f(j)), featb.at[1, source])
        )
    featb[1, f] = featb[0, f]

    lhs = jnp.concatenate(
        [shifted(down, 1).astype(BF16), down_own, shifted(down, -1).astype(BF16)], axis=0
    )
    terms = nt_dot(lhs, around)

    def deal(values, height, buffer, per, step):
        for g in range(n_f):
            tiles = [
                values[per * g + step * r : per * g + step * r + height, 128 * c : 128 * c + 128]
                for r in range(3)
                for c in range(5)
            ]
            tiles.append(jnp.zeros((height, 128), F32))
            for half in range(2):
                piece = jnp.concatenate(tiles[8 * half : 8 * half + 8], axis=0)
                buffer[half, g] = piece.astype(BF16)

    deal(terms, 16, s_gb, 16, 128)

    def to_twin(gb, cb):
        return [(send(gb.at[1 - core], cb, twin), cb)]

    def over_filt(gb, cb, pb, fb):
        pb[...] = (gb[core].astype(F32) + cb[...].astype(F32)).astype(BF16)
        fb[f] = pb[f]
        waits = []
        for j in range(1, n_f):
            other = lax.rem(f + j, n_f)
            source = lax.rem(f - j + n_f, n_f)
            waits.append((send(pb.at[other], fb.at[f], along_f(j)), fb.at[source]))
        return waits

    def summed(ref, count):
        value = ref[0].astype(F32)
        for k in range(1, count):
            value = value + ref[k].astype(F32)
        return value.astype(BF16)

    def over_y(fb, yr):
        yr[y] = summed(fb, n_f)
        waits = []
        for j in range(1, n_y):
            source = lax.rem(y - j + n_y, n_y)
            waits.append((send(yr.at[y], yr.at[y], along_y(j)), yr.at[source]))
        return waits

    def over_z(yr, zr):
        zr[zh] = summed(yr, n_y)
        waits = []
        for j in range(1, n_z):
            source = lax.rem(zh - j + n_z, n_z)
            waits.append((send(zr.at[zh], zr.at[zh], along_z(j)), zr.at[source]))
        return waits

    s_waits = to_twin(s_gb, s_cb)

    finish(s_waits)
    s_waits = over_filt(s_gb, s_cb, s_pb, s_fb)

    finish(down_waits)
    zero_rim(take, 2)
    pool_grad = own_share
    for dx, dy in DIRS:
        pool_grad = pool_grad + take[1 - dx, 1 - dy].astype(F32)
    pool_grad = 0.125 * pool_grad
    high = pool_grad.astype(BF16)
    low = (pool_grad - high.astype(F32)).astype(BF16)
    spread = nt_dot(jnp.concatenate([high, low], axis=0), pairs)
    spread = spread[0:64] + spread[64:128]
    for a in range(2):
        for b in range(2):
            extd[a + 1, b + 1] = (spread * slope1[a, b]).astype(BF16)
    fd_waits = halo_start(extd)

    terms = jnp.zeros((192, 640), F32)
    for a in range(2):
        for b in range(2):
            own = extd[a + 1, b + 1]
            wide = own.astype(F32)
            lhs = jnp.concatenate(
                [shifted(wide, 1).astype(BF16), own, shifted(wide, -1).astype(BF16)], axis=0
            )
            terms = terms + nt_dot(lhs, stack(ext, a, b))
    deal(terms, 8, f_gb, 24, 8)
    f_waits = to_twin(f_gb, f_cb)

    finish(s_waits)
    s_waits = over_y(s_fb, s_yr)
    finish(f_waits)
    f_waits = over_filt(f_gb, f_cb, f_pb, f_fb)
    finish(s_waits)
    s_waits = over_z(s_yr, s_zr)

    finish(fd_waits)
    zero_rim(extd, 3)
    wb = w1b[...]
    for a in range(2):
        for b in range(2):
            rows = jnp.dot(wb, stack(extd, a, b), preferred_element_type=F32)
            plane = shifted(rows[0:64], 1) + rows[64:128] + shifted(rows[128:192], -1)
            for h in range(2):
                vrows[h, pl.ds(2 * a + b, 64, stride=4), :] = plane[:, 128 * h : 128 * h + 128]

    finish(f_waits)
    f_waits = over_y(f_fb, f_yr)

    for c in range(64):
        for a in range(2):
            for h in range(2):
                vgrad_out[c, a, :, 128 * h : 128 * h + 128] = vrows[
                    h, 4 * c + 2 * a : 4 * c + 2 * a + 2
                ].astype(BF16)

    finish(f_waits)
    f_waits = over_z(f_yr, f_zr)

    finish(s_waits)
    s_os[core] = summed(s_zr, n_z)
    s_waits = [(send(s_os.at[core], s_os.at[core], twin), s_os.at[1 - core])]
    finish(feat_waits)
    for k in range(n_f):
        crows[pl.ds(k, 16, stride=n_f), :] = featb[1, k].astype(F32)
    feat_out[...] = crows[...].reshape(16, 1, n_f, 128).astype(BF16)
    finish(s_waits)
    os_out[...] = s_os[...]

    finish(f_waits)
    f_ag[core, f] = summed(f_zr, n_z)
    f_waits = []
    for j in range(1, n_f):
        source = lax.rem(f - j + n_f, n_f)
        f_waits.append((send(f_ag.at[core, f], f_ag.at[core, f], along_f(j)), f_ag.at[core, source]))
    finish(f_waits)
    f_waits = [(send(f_ag.at[core], f_ag.at[core], twin), f_ag.at[1 - core])]
    finish(f_waits)
    ag_out[...] = f_ag[...]

    for copy in sent:
        copy.wait_send()


def unpack(n_f, scales, feat_in, vgrad_in, ag_in, os_in, feat_out, vgrad_out, g1_out, g2_out):
    fine_scale, bottom_scale = scales
    feat_out[...] = feat_in[...]
    vgrad_out[...] = vgrad_in[...]
    for k in range(15):
        dz, c = k // 5, k % 5
        tile = os_in[k // 8, 16 * (k % 8) : 16 * (k % 8) + 16].astype(F32) * bottom_scale
        g2_out[6 * c + dz] = tile[:, 0:64]
        if c < 4:
            g2_out[6 * c + 3 + dz] = pltpu.roll(tile, 64, 1)[:, 0:64]
    for g in range(n_f):
        both = [ag_in[h, g].astype(F32) * fine_scale for h in range(2)]
        for k in range(15):
            row = 24 * g + 8 * (k // 5)
            dz, o = row // 64, row % 64
            c = k % 5
            tile = both[k // 8][8 * (k % 8) : 8 * (k % 8) + 8]
            g1_out[6 * c + dz, o : o + 8] = tile[:, 0:64]
            if c < 4:
                g1_out[6 * c + 3 + dz, o : o + 8] = pltpu.roll(tile, 64, 1)[:, 0:64]


def local(sizes, volume, first_weight, second_weight, cotangent):
    n_s, n_f, n_y, n_z = sizes
    scales = (
        1.0 / float(n_s * 2 * n_f * 2 * 256) ** 0.5,
        1.0 / float(n_s * n_f * 128) ** 0.5,
    )
    vmem = pl.BlockSpec(memory_space=pltpu.VMEM)
    whole = pl.BlockSpec(memory_space=pltpu.HBM)
    operands = (volume, cotangent, first_weight, second_weight)
    shape = jax.ShapeDtypeStruct
    features, volume_grad, fine, bottom = pl.pallas_call(
        functools.partial(kernel, sizes),
        out_shape=(
            shape((16, 1, n_f, 128), BF16),
            shape((64, 2, 2, 256), BF16),
            shape((2, n_f, 64, 128), BF16),
            shape((2, 128, 128), BF16),
        ),
        in_specs=[whole] * 4,
        out_specs=(vmem,) * 4,
        scratch_shapes=[
            pltpu.VMEM((64, 2, 2, 256), BF16),
            pltpu.VMEM((16, 1, n_f, 128), BF16),
            pltpu.VMEM((27, 64, 64), BF16),
            pltpu.VMEM((27, 16, 64), BF16),
            pltpu.VMEM((2, 256, 128), F32),
            pltpu.VMEM((16 * n_f, 128), F32),
            pltpu.VMEM((n_f, 16, 128), BF16),
            pltpu.VMEM((192, 640), BF16),
            pltpu.VMEM((192, 640), BF16),
            pltpu.VMEM((16, 16, 128), BF16),
            pltpu.VMEM((4, 4, 64, 256), BF16),
            pltpu.VMEM((4, 4, 64, 256), BF16),
            pltpu.VMEM((2, 2, 64, 256), F32),
            pltpu.VMEM((n_f, 16, 128), BF16),
            pltpu.VMEM((2, n_f, 8, 16, 128), BF16),
            pltpu.VMEM((3, 640, 128), BF16),
            pltpu.VMEM((4, 3, 64, 128), BF16),
            pltpu.VMEM((9, 64, 128), BF16),
            pltpu.VMEM((3, 3, 64, 128), BF16),
            pltpu.VMEM((2, n_f, 16, 128), BF16),
            pltpu.VMEM((2, n_f, 128, 128), BF16),
            pltpu.VMEM((n_f, 128, 128), BF16),
            pltpu.VMEM((n_f, 128, 128), BF16),
            pltpu.VMEM((n_f, 128, 128), BF16),
            pltpu.VMEM((n_y, 128, 128), BF16),
            pltpu.VMEM((n_z, 128, 128), BF16),
            pltpu.VMEM((2, 128, 128), BF16),
            pltpu.VMEM((2, n_f, 64, 128), BF16),
            pltpu.VMEM((n_f, 64, 128), BF16),
            pltpu.VMEM((n_f, 64, 128), BF16),
            pltpu.VMEM((n_f, 64, 128), BF16),
            pltpu.VMEM((n_y, 64, 128), BF16),
            pltpu.VMEM((n_z, 64, 128), BF16),
            pltpu.VMEM((2, n_f, 64, 128), BF16),
            pltpu.SemaphoreType.DMA((4,)),
            pltpu.SemaphoreType.DMA((N_SEMS,)),
            pltpu.SemaphoreType.DMA((N_SEMS,)),
        ],
        compiler_params=pltpu.CompilerParams(
            collective_id=0, has_side_effects=True, vmem_limit_bytes=24 * 1024 * 1024
        ),
        name="block",
    )(*(pltpu.with_memory_space_constraint(v, pltpu.HBM) for v in operands))
    return pl.pallas_call(
        functools.partial(unpack, n_f, scales),
        out_shape=(
            shape((16, 1, n_f, 128), BF16),
            shape((64, 2, 2, 256), BF16),
            shape((27, 64, 64), F32),
            shape((27, 16, 64), F32),
        ),
        in_specs=[vmem] * 4,
        out_specs=(vmem,) * 4,
        compiler_params=pltpu.CompilerParams(vmem_limit_bytes=24 * 1024 * 1024),
        name="unpack",
    )(features, volume_grad, fine, bottom)


def solution(mesh):
    n_s, n_f = mesh.shape["space"], mesh.shape["filt"]
    n_z = 4 if n_s % 8 == 0 else 1
    sizes = (n_s, n_f, n_s // (2 * n_z), n_z)
    placed = (
        P(None, "space", "filt", None),
        P(),
        P(None, "filt", None),
        P("filt", "space", None, None),
    )
    return jax.shard_map(
        functools.partial(local, sizes),
        mesh=mesh,
        in_specs=placed,
        out_specs=(
            P("filt", "space", None, None),
            P(None, "space", "filt", None),
            P(),
            P(None, "filt", None),
        ),
        check_vma=False,
    )
```

time: 79.7 us -> 61.1 us (0.77)
  local copies, waits for them, and re-layouts: 14.2 us -> 0 us
  Pallas kernels: 64.6 us -> 60.4 us
    unnamed x12 -> x0, local copies, waits for them, and re-layouts: 9.03 us -> none
    pallas_call x1 -> x2, Pallas kernels: 64.6 us -> 60.4 us  [the longest x1 59.2 us: local(): pl.pallas_call(functools.partial(kernel, sizes), out_shape=(shape((16, 1,...]
    reshape x8 -> x0, local copies, waits for them, and re-layouts: 2.88 us -> none  [the longest x2 1.6 us: local(): taps = first_weight.reshape(9, 3, 64, 64)]
    pad x3 -> x0, local copies, waits for them, and re-layouts: 2.08 us -> none  [the longest x1 0.72 us: local(): w1f = jnp.pad(jnp.transpose(taps, (1, 2, 0, 3)).reshape(192, 576), pad)]
where the time goes in v2:
time: 61.1 us; the launch traced here: 61 us
  Pallas kernels  60.4 us (99%)
  between operations  0.64 us (1%)
    pallas_call x1, Pallas kernels, local(): pl.pallas_call(functools.partial(kernel, sizes), out_shape=(shape((16, 1,...  59.2 us

profile of v2, /device:TPU:1, one launch (start us, length us, event | category | flops | bytes accessed | tf_op | source)
XLA Modules:
  0.0 61.0 jit_solution(297713828378831296)
XLA Ops:
  0.6 59.2 %block.1 = (bf16[16,1,8,128]{3,2,1,0:T(8,128)(2,1)S(1)}, bf16[64,2,2,256]{3,2,1,0:T(2,128)(2,1)S(1)}, bf16[2,8,64,128]{3,2,1,0:T(8,128)(2,1)S(1)}, bf16[2,128,128]{2,1,0:T(8,128)(2,1)S(1)}) custom-call(bf16[64,2,2,256]{3,2,1,0:T(2,128)(2,1)} %vol_hbm.1, bf16[16,1,8,128]{3,2,1,0:T(8,128)(2,1)} %cot_hbm.1, bf16[27,64,64]{2,1,0:T(8,128)(2,1)} %w1_hbm.1, ...), custom_call_target="tpu_custom_call" | custom-call | tf_op jit(solution)/shard_map/block/pallas_call | solution.py:482
  59.8 1.2 %unpack.1 = (bf16[16,1,8,128]{3,2,1,0:T(8,128)(2,1)}, bf16[64,2,2,256]{3,2,1,0:T(2,128)(2,1)}, f32[27,64,64]{2,1,0:T(8,128)}, f32[27,16,64]{2,1,0:T(8,128)}) custom-call(bf16[16,1,8,128]{3,2,1,0:T(8,128)(2,1)S(1)} %get-tuple-element.8.feat_in, bf16[64,2,2,256]{3,2,1,0:T(2,128)(2,1)S(1)} %get-tuple-element.9.vgrad_in, ...), custom_call_target="tpu_custom_call" | custom-call | tf_op jit(solution)/shard_map/unpack/pallas_call | solution.py:536

commit v3 on v2

--- a/solution.py
+++ b/solution.py
@@ -10,8 +10,8 @@
 MESH = pl.DeviceIdType.MESH
 F32 = jnp.float32
 BF16 = jnp.bfloat16
-DIRS = [(dx, dy) for dx in (-1, 0, 1) for dy in (-1, 0, 1) if (dx, dy) != (0, 0)]
-N_SEMS = 128
+DIRS = [(-1, -1), (-1, 1), (1, -1), (1, 1), (-1, 0), (1, 0), (0, -1), (0, 1)]
+N_SEMS = 108
 
 
 def sigmoid(v):
@@ -76,8 +76,7 @@
     f_gb,
     f_cb,
     f_pb,
-    f_fb,
-    f_yr,
+    f_xr,
     f_zr,
     f_ag,
     load_sem,
@@ -112,12 +111,39 @@
         return ((y * n_z + lax.rem(zh + j, n_z)) * 2 + core, f)
 
     twin = (s + 1 - 2 * core, f)
-
-    peers = [near(dx, dy) for dx, dy in DIRS]
-    peers += [along_f(j) for j in range(1, n_f)]
-    peers += [along_y(j) for j in range(1, n_y)]
-    peers += [along_z(j) for j in range(1, n_z)]
-    peers += [twin]
+    n_x = n_f // 2
+    n_xy = n_x * n_y
+    x, zl = lax.rem(f, n_x), f // n_x
+    at_xy = y * n_x + x
+    at_z = 2 * zh + zl
+
+    def over_plane(j):
+        to = lax.rem(at_xy + j, n_xy)
+        return ((to // n_x * n_z + zh) * 2 + core, zl * n_x + lax.rem(to, n_x))
+
+    def over_depth(j):
+        to = lax.rem(at_z + j, 2 * n_z)
+        return ((y * n_z + to // 2) * 2 + core, lax.rem(to, 2) * n_x + x)
+
+    to_f = [along_f(j) for j in range(1, n_f)]
+    to_y = [along_y(j) for j in range(1, n_y)]
+    to_z = [along_z(j) for j in range(1, n_z)]
+    to_plane = [over_plane(j) for j in range(1, n_xy)]
+    to_depth = [over_depth(j) for j in range(1, 2 * n_z)]
+
+    def ahead(me, count):
+        return [lax.rem(me + j, count) for j in range(1, count)]
+
+    def behind(me, count):
+        return [lax.rem(me - j + count, count) for j in range(1, count)]
+
+    f_ahead, f_behind = ahead(f, n_f), behind(f, n_f)
+    y_behind, z_behind = behind(y, n_y), behind(zh, n_z)
+    plane_ahead, plane_behind = ahead(at_xy, n_xy), behind(at_xy, n_xy)
+    depth_behind = behind(at_z, 2 * n_z)
+    first, second = core == 0, core == 1
+
+    peers = [near(dx, dy) for dx, dy in DIRS] + to_f + to_plane + to_depth
     barrier = pltpu.get_barrier_semaphore()
     for peer in peers:
         pl.semaphore_signal(barrier, inc=1, device_id=peer, device_id_type=MESH)
@@ -138,9 +164,11 @@
     pl.semaphore_wait(barrier, len(peers))
 
     sent = []
-
-    def send(src, dst, device):
+    groups = {}
+
+    def send(src, dst, device, only=None, size=None):
         at = len(sent)
+        groups.setdefault(only, []).append((at, size or (lambda: src)))
         copy = pltpu.make_async_remote_copy(
             src_ref=src,
             dst_ref=dst,
@@ -154,7 +182,13 @@
         return at
 
     def arrive(ref, at):
+        ref = ref() if callable(ref) else ref
         pltpu.make_async_copy(ref, ref, recv_sem.at[at]).wait()
+
+    def drain(only):
+        for at, size in groups[only]:
+            ref = size()
+            pltpu.make_async_copy(ref, ref, send_sem.at[at]).wait()
 
     def src_part(d):
         return {1: 2, -1: 1, 0: slice(1, 3)}[d]
@@ -311,7 +345,7 @@
     )
     terms = nt_dot(lhs, around)
 
-    def deal(values, height, buffer, per, step):
+    def deal(values, height, per, step, put):
         for g in range(n_f):
             tiles = [
                 values[per * g + step * r : per * g + step * r + height, 128 * c : 128 * c + 128]
@@ -319,24 +353,30 @@
                 for c in range(5)
             ]
             tiles.append(jnp.zeros((height, 128), F32))
-            for half in range(2):
-                piece = jnp.concatenate(tiles[8 * half : 8 * half + 8], axis=0)
-                buffer[half, g] = piece.astype(BF16)
-
-    deal(terms, 16, s_gb, 16, 128)
-
-    def to_twin(gb, cb):
-        return [(send(gb.at[1 - core], cb, twin), cb)]
-
-    def over_filt(gb, cb, pb, fb):
-        pb[...] = (gb[core].astype(F32) + cb[...].astype(F32)).astype(BF16)
-        fb[f] = pb[f]
-        waits = []
-        for j in range(1, n_f):
-            other = lax.rem(f + j, n_f)
-            source = lax.rem(f - j + n_f, n_f)
-            waits.append((send(pb.at[other], fb.at[f], along_f(j)), fb.at[source]))
-        return waits
+            put(g, jnp.concatenate(tiles, axis=0).astype(BF16))
+
+    def put_bottom(g, piece):
+        s_gb[g] = piece
+
+    deal(terms, 16, 16, 128, put_bottom)
+
+    def exchange(ref, mine, peers, sources, only):
+        return [
+            (
+                send(ref.at[mine], ref.at[mine], peer, only, lambda: ref.at[mine]),
+                lambda source=source: ref.at[source],
+            )
+            for peer, source in zip(peers, sources)
+        ]
+
+    def scatter(out, into, mine, peers, theirs, sources, only):
+        return [
+            (
+                send(out.at[other], into.at[mine], peer, only, lambda other=other: out.at[other]),
+                lambda source=source: into.at[source],
+            )
+            for peer, other, source in zip(peers, theirs, sources)
+        ]
 
     def summed(ref, count):
         value = ref[0].astype(F32)
@@ -344,26 +384,20 @@
             value = value + ref[k].astype(F32)
         return value.astype(BF16)
 
-    def over_y(fb, yr):
-        yr[y] = summed(fb, n_f)
-        waits = []
-        for j in range(1, n_y):
-            source = lax.rem(y - j + n_y, n_y)
-            waits.append((send(yr.at[y], yr.at[y], along_y(j)), yr.at[source]))
-        return waits
-
-    def over_z(yr, zr):
-        zr[zh] = summed(yr, n_y)
-        waits = []
-        for j in range(1, n_z):
-            source = lax.rem(zh - j + n_z, n_z)
-            waits.append((send(zr.at[zh], zr.at[zh], along_z(j)), zr.at[source]))
-        return waits
-
-    s_waits = to_twin(s_gb, s_cb)
-
-    finish(s_waits)
-    s_waits = over_filt(s_gb, s_cb, s_pb, s_fb)
+    s_waits, f_waits = [], []
+
+    @pl.when(second)
+    def _():
+        send(s_gb, s_cb, twin, 1)
+
+    s_twin = len(sent) - 1
+
+    @pl.when(first)
+    def _():
+        arrive(s_cb, s_twin)
+        s_pb[...] = (s_gb[...].astype(F32) + s_cb[...].astype(F32)).astype(BF16)
+        s_fb[f] = s_pb[f]
+        s_waits.extend(scatter(s_pb, s_fb, f, to_f, f_ahead, f_behind, 0))
 
     finish(down_waits)
     zero_rim(take, 2)
@@ -389,15 +423,38 @@
                 [shifted(wide, 1).astype(BF16), own, shifted(wide, -1).astype(BF16)], axis=0
             )
             terms = terms + nt_dot(lhs, stack(ext, a, b))
-    deal(terms, 8, f_gb, 24, 8)
-    f_waits = to_twin(f_gb, f_cb)
-
-    finish(s_waits)
-    s_waits = over_y(s_fb, s_yr)
-    finish(f_waits)
-    f_waits = over_filt(f_gb, f_cb, f_pb, f_fb)
-    finish(s_waits)
-    s_waits = over_z(s_yr, s_zr)
+
+    per_peer = 16 // n_xy
+
+    def put_fine(g, piece):
+        for h in range(2):
+            at = 2 * g + h
+            row = 64 * (at % per_peer)
+            f_gb[at // per_peer, row : row + 64] = piece[64 * h : 64 * h + 64]
+
+    deal(terms, 8, 24, 8, put_fine)
+
+    @pl.when(first)
+    def _():
+        send(f_gb, f_cb, twin, 0)
+
+    f_twin = len(sent) - 1
+    plane_waits, y_waits = [], []
+
+    @pl.when(second)
+    def _():
+        arrive(f_cb, f_twin)
+        f_pb[...] = (f_gb[...].astype(F32) + f_cb[...].astype(F32)).astype(BF16)
+        f_xr[at_xy] = f_pb[at_xy]
+        plane_waits.extend(
+            scatter(f_pb, f_xr, at_xy, to_plane, plane_ahead, plane_behind, 1)
+        )
+
+    @pl.when(first)
+    def _():
+        finish(s_waits)
+        s_yr[y] = summed(s_fb, n_f)
+        y_waits.extend(exchange(s_yr, y, to_y, y_behind, 0))
 
     finish(fd_waits)
     zero_rim(extd, 3)
@@ -409,9 +466,6 @@
             for h in range(2):
                 vrows[h, pl.ds(2 * a + b, 64, stride=4), :] = plane[:, 128 * h : 128 * h + 128]
 
-    finish(f_waits)
-    f_waits = over_y(f_fb, f_yr)
-
     for c in range(64):
         for a in range(2):
             for h in range(2):
@@ -419,32 +473,60 @@
                     h, 4 * c + 2 * a : 4 * c + 2 * a + 2
                 ].astype(BF16)
 
-    finish(f_waits)
-    f_waits = over_z(f_yr, f_zr)
-
-    finish(s_waits)
-    s_os[core] = summed(s_zr, n_z)
-    s_waits = [(send(s_os.at[core], s_os.at[core], twin), s_os.at[1 - core])]
+    depth_waits, z_waits = [], []
+
+    @pl.when(second)
+    def _():
+        finish(plane_waits)
+        f_zr[at_z] = summed(f_xr, n_xy)
+        depth_waits.extend(exchange(f_zr, at_z, to_depth, depth_behind, 1))
+
+    @pl.when(first)
+    def _():
+        finish(y_waits)
+        s_zr[zh] = summed(s_yr, n_y)
+        z_waits.extend(exchange(s_zr, zh, to_z, z_behind, 0))
+
     finish(feat_waits)
     for k in range(n_f):
         crows[pl.ds(k, 16, stride=n_f), :] = featb[1, k].astype(F32)
     feat_out[...] = crows[...].reshape(16, 1, n_f, 128).astype(BF16)
-    finish(s_waits)
+
+    @pl.when(first)
+    def _():
+        finish(z_waits)
+        s_os[...] = summed(s_zr, n_z)
+        send(s_os, s_os, twin, 0)
+
+    s_last = len(sent) - 1
+
+    @pl.when(second)
+    def _():
+        finish(depth_waits)
+        f_ag[at_xy] = summed(f_zr, 2 * n_z)
+        finish(exchange(f_ag, at_xy, to_plane, plane_behind, 1))
+        send(f_ag, f_ag, twin, 1)
+        arrive(s_os, s_last)
+
+    f_last = len(sent) - 1
+
+    @pl.when(first)
+    def _():
+        arrive(f_ag, f_last)
+
     os_out[...] = s_os[...]
-
-    finish(f_waits)
-    f_ag[core, f] = summed(f_zr, n_z)
-    f_waits = []
-    for j in range(1, n_f):
-        source = lax.rem(f - j + n_f, n_f)
-        f_waits.append((send(f_ag.at[core, f], f_ag.at[core, f], along_f(j)), f_ag.at[core, source]))
-    finish(f_waits)
-    f_waits = [(send(f_ag.at[core], f_ag.at[core], twin), f_ag.at[1 - core])]
-    finish(f_waits)
     ag_out[...] = f_ag[...]
 
-    for copy in sent:
-        copy.wait_send()
+    assert len(sent) <= N_SEMS
+    drain(None)
+
+    @pl.when(first)
+    def _():
+        drain(0)
+
+    @pl.when(second)
+    def _():
+        drain(1)
 
 
 def unpack(n_f, scales, feat_in, vgrad_in, ag_in, os_in, feat_out, vgrad_out, g1_out, g2_out):
@@ -453,12 +535,16 @@
     vgrad_out[...] = vgrad_in[...]
     for k in range(15):
         dz, c = k // 5, k % 5
-        tile = os_in[k // 8, 16 * (k % 8) : 16 * (k % 8) + 16].astype(F32) * bottom_scale
+        tile = os_in[16 * k : 16 * k + 16].astype(F32) * bottom_scale
         g2_out[6 * c + dz] = tile[:, 0:64]
         if c < 4:
             g2_out[6 * c + 3 + dz] = pltpu.roll(tile, 64, 1)[:, 0:64]
     for g in range(n_f):
-        both = [ag_in[h, g].astype(F32) * fine_scale for h in range(2)]
+        per_peer = 16 // ag_in.shape[0]
+        both = []
+        for at in (2 * g, 2 * g + 1):
+            start = 64 * (at % per_peer)
+            both.append(ag_in[at // per_peer, start : start + 64].astype(F32) * fine_scale)
         for k in range(15):
             row = 24 * g + 8 * (k // 5)
             dz, o = row // 64, row % 64
@@ -471,6 +557,7 @@
 
 def local(sizes, volume, first_weight, second_weight, cotangent):
     n_s, n_f, n_y, n_z = sizes
+    n_xy = n_f // 2 * n_y
     scales = (
         1.0 / float(n_s * 2 * n_f * 2 * 256) ** 0.5,
         1.0 / float(n_s * n_f * 128) ** 0.5,
@@ -484,8 +571,8 @@
         out_shape=(
             shape((16, 1, n_f, 128), BF16),
             shape((64, 2, 2, 256), BF16),
-            shape((2, n_f, 64, 128), BF16),
-            shape((2, 128, 128), BF16),
+            shape((n_xy, 1024 // n_xy, 128), BF16),
+            shape((256, 128), BF16),
         ),
         in_specs=[whole] * 4,
         out_specs=(vmem,) * 4,
@@ -510,20 +597,19 @@
             pltpu.VMEM((9, 64, 128), BF16),
             pltpu.VMEM((3, 3, 64, 128), BF16),
             pltpu.VMEM((2, n_f, 16, 128), BF16),
-            pltpu.VMEM((2, n_f, 128, 128), BF16),
-            pltpu.VMEM((n_f, 128, 128), BF16),
-            pltpu.VMEM((n_f, 128, 128), BF16),
-            pltpu.VMEM((n_f, 128, 128), BF16),
-            pltpu.VMEM((n_y, 128, 128), BF16),
-            pltpu.VMEM((n_z, 128, 128), BF16),
-            pltpu.VMEM((2, 128, 128), BF16),
-            pltpu.VMEM((2, n_f, 64, 128), BF16),
-            pltpu.VMEM((n_f, 64, 128), BF16),
-            pltpu.VMEM((n_f, 64, 128), BF16),
-            pltpu.VMEM((n_f, 64, 128), BF16),
-            pltpu.VMEM((n_y, 64, 128), BF16),
-            pltpu.VMEM((n_z, 64, 128), BF16),
-            pltpu.VMEM((2, n_f, 64, 128), BF16),
+            pltpu.VMEM((n_f, 256, 128), BF16),
+            pltpu.VMEM((n_f, 256, 128), BF16),
+            pltpu.VMEM((n_f, 256, 128), BF16),
+            pltpu.VMEM((n_f, 256, 128), BF16),
+            pltpu.VMEM((n_y, 256, 128), BF16),
+            pltpu.VMEM((n_z, 256, 128), BF16),
+            pltpu.VMEM((256, 128), BF16),
+            pltpu.VMEM((n_xy, 1024 // n_xy, 128), BF16),
+            pltpu.VMEM((n_xy, 1024 // n_xy, 128), BF16),
+            pltpu.VMEM((n_xy, 1024 // n_xy, 128), BF16),
+            pltpu.VMEM((n_xy, 1024 // n_xy, 128), BF16),
+            pltpu.VMEM((2 * n_z, 1024 // n_xy, 128), BF16),
+            pltpu.VMEM((n_xy, 1024 // n_xy, 128), BF16),
             pltpu.SemaphoreType.DMA((4,)),
             pltpu.SemaphoreType.DMA((N_SEMS,)),
             pltpu.SemaphoreType.DMA((N_SEMS,)),

time: 61.1 us -> 54.4 us (0.89)
  Pallas kernels: 60.4 us -> 53.7 us
    pallas_call x1, Pallas kernels: 59.2 us -> 52.5 us  [local(): pl.pallas_call(functools.partial(kernel, sizes), out_shape=(shape((16, 1,...]
where the time goes in v3:
time: 54.4 us; the launch traced here: 54.3 us
  Pallas kernels  53.7 us (99%)
  between operations  0.64 us (1%)
    pallas_call x1, Pallas kernels, local(): pl.pallas_call(functools.partial(kernel, sizes), out_shape=(shape((16, 1,...  52.5 us
    pallas_call x1, Pallas kernels, local(): pl.pallas_call(functools.partial(unpack, n_f, scales), out_shape=(shape((...  1.17 us

profile of v3, /device:TPU:1, one launch (start us, length us, event | category | flops | bytes accessed | tf_op | source)
XLA Modules:
  0.0 54.3 jit_solution(6170367287743573110)
XLA Ops:
  0.6 52.5 %block.1 = (bf16[16,1,8,128]{3,2,1,0:T(8,128)(2,1)S(1)}, bf16[64,2,2,256]{3,2,1,0:T(2,128)(2,1)S(1)}, bf16[16,64,128]{2,1,0:T(8,128)(2,1)S(1)}, bf16[256,128]{1,0:T(8,128)(2,1)S(1)}) custom-call(bf16[64,2,2,256]{3,2,1,0:T(2,128)(2,1)} %vol_hbm.1, bf16[16,1,8,128]{3,2,1,0:T(8,128)(2,1)} %cot_hbm.1, bf16[27,64,64]{2,1,0:T(8,128)(2,1)} %w1_hbm.1, ...), custom_call_target="tpu_custom_call" | custom-call | tf_op jit(solution)/shard_map/block/pallas_call | solution.py:569
  53.1 1.2 %unpack.1 = (bf16[16,1,8,128]{3,2,1,0:T(8,128)(2,1)}, bf16[64,2,2,256]{3,2,1,0:T(2,128)(2,1)}, f32[27,64,64]{2,1,0:T(8,128)}, f32[27,16,64]{2,1,0:T(8,128)}) custom-call(bf16[16,1,8,128]{3,2,1,0:T(8,128)(2,1)S(1)} %get-tuple-element.8.feat_in, bf16[64,2,2,256]{3,2,1,0:T(2,128)(2,1)S(1)} %get-tuple-element.9.vgrad_in, ...), custom_call_target="tpu_custom_call" | custom-call | tf_op jit(solution)/shard_map/unpack/pallas_call | solution.py:622

commit v4 on v3

--- a/solution.py
+++ b/solution.py
@@ -11,7 +11,7 @@
 F32 = jnp.float32
 BF16 = jnp.bfloat16
 DIRS = [(-1, -1), (-1, 1), (1, -1), (1, 1), (-1, 0), (1, 0), (0, -1), (0, 1)]
-N_SEMS = 108
+N_SEMS = 130
 
 
 def sigmoid(v):
@@ -142,8 +142,15 @@
     plane_ahead, plane_behind = ahead(at_xy, n_xy), behind(at_xy, n_xy)
     depth_behind = behind(at_z, 2 * n_z)
     first, second = core == 0, core == 1
-
-    peers = [near(dx, dy) for dx, dy in DIRS] + to_f + to_plane + to_depth
+    in_s = {-1: s > 0, 0: s >= 0, 1: s < n_s - 1}
+    in_f = {-1: f > 0, 0: f >= 0, 1: f < n_f - 1}
+    exists = {(dx, dy): in_s[dx] & in_f[dy] for dx, dy in DIRS}
+    beside = {d: near(*d) for d in DIRS}
+    flip = (1 - zl) * n_x + x
+    x_ahead = [zl * n_x + lax.rem(x + j, n_x) for j in range(1, n_x)]
+    x_behind = [lax.rem(x - j + n_x, n_x) for j in range(1, n_x)]
+
+    peers = [beside[d] for d in DIRS] + to_f + to_plane + to_depth
     barrier = pltpu.get_barrier_semaphore()
     for peer in peers:
         pl.semaphore_signal(barrier, inc=1, device_id=peer, device_id_type=MESH)
@@ -198,11 +205,28 @@
 
     def halo_start(field):
         out = []
-        for dx, dy in DIRS:
-            target = field.at[dst_part(dx), dst_part(dy)]
-            source = field.at[src_part(dx), src_part(dy)]
-            out.append((send(source, target, near(dx, dy)), target))
+        for d in DIRS:
+            dx, dy = d
+
+            def source(dx=dx, dy=dy):
+                return field.at[src_part(dx), src_part(dy)]
+
+            def target(dx=dx, dy=dy):
+                return field.at[dst_part(dx), dst_part(dy)]
+
+            @pl.when(exists[d])
+            def _(d=d, source=source, target=target):
+                send(source(), target(), beside[d], d, source)
+
+            out.append((d, len(sent) - 1, target))
         return out
+
+    def halo_finish(waits):
+        for (dx, dy), at, target in waits:
+
+            @pl.when(exists[-dx, -dy])
+            def _(at=at, target=target):
+                arrive(target, at)
 
     def finish(waits):
         for at, ref in waits:
@@ -230,6 +254,8 @@
                 field[a, last] = jnp.zeros(field.shape[2:], field.dtype)
 
     vol_waits = halo_start(ext)
+    zero_rim(ext, 3)
+    zero_rim(extd, 3)
 
     loads[1].wait()
     for k in range(15):
@@ -238,10 +264,11 @@
         w2p[k] = side_by_side(w2raw[6 * c + dz], right)
     w2p[15] = jnp.zeros((16, 128), BF16)
     half = w2p.at[pl.ds(8 * core, 8)]
+    w2_flip = send(half, w2g.at[core, f], (s, flip))
     w2_waits = []
-    for j in range(1, n_f):
-        source = lax.rem(f - j + n_f, n_f)
-        w2_waits.append((send(half, w2g.at[core, f], along_f(j)), w2g.at[core, source]))
+    for j, to in enumerate(x_ahead):
+        source = zl * n_x + x_behind[j]
+        w2_waits.append((send(half, w2g.at[core, f], (s, to)), w2g.at[core, source]))
     w2g[core, f] = w2p[pl.ds(8 * core, 8)]
 
     loads[2].wait()
@@ -275,8 +302,12 @@
         planes = [field[a + i, b + j] for i in range(3) for j in range(3)]
         return jnp.concatenate(planes + [jnp.zeros((64, 256), BF16)], axis=0)
 
-    finish(vol_waits)
-    zero_rim(ext, 3)
+    arrive(w2g.at[core, flip], w2_flip)
+    for j, to in enumerate(x_ahead):
+        mine = w2g.at[core, flip]
+        source = (1 - zl) * n_x + x_behind[j]
+        w2_waits.append((send(mine, mine, (s, to)), w2g.at[core, source]))
+    halo_finish(vol_waits)
 
     wf = w1f[...]
     total = jnp.zeros((64, 128), F32)
@@ -432,18 +463,24 @@
             row = 64 * (at % per_peer)
             f_gb[at // per_peer, row : row + 64] = piece[64 * h : 64 * h + 64]
 
+        def part(buffer):
+            if per_peer == 1:
+                return buffer.at[2 * g : 2 * g + 2]
+            return buffer.at[2 * g // per_peer, pl.ds(64 * (2 * g % per_peer), 128)]
+
+        @pl.when(first)
+        def _():
+            send(part(f_gb), part(f_cb), twin, 0, lambda: part(f_gb))
+
+        f_twin.append((len(sent) - 1, lambda: part(f_cb)))
+
+    f_twin = []
     deal(terms, 8, 24, 8, put_fine)
-
-    @pl.when(first)
-    def _():
-        send(f_gb, f_cb, twin, 0)
-
-    f_twin = len(sent) - 1
-    plane_waits, y_waits = [], []
+    plane_waits, z_waits = [], []
 
     @pl.when(second)
     def _():
-        arrive(f_cb, f_twin)
+        finish(f_twin)
         f_pb[...] = (f_gb[...].astype(F32) + f_cb[...].astype(F32)).astype(BF16)
         f_xr[at_xy] = f_pb[at_xy]
         plane_waits.extend(
@@ -453,11 +490,10 @@
     @pl.when(first)
     def _():
         finish(s_waits)
-        s_yr[y] = summed(s_fb, n_f)
-        y_waits.extend(exchange(s_yr, y, to_y, y_behind, 0))
-
-    finish(fd_waits)
-    zero_rim(extd, 3)
+        s_zr[zh] = summed(s_fb, n_f)
+        z_waits.extend(exchange(s_zr, zh, to_z, z_behind, 0))
+
+    halo_finish(fd_waits)
     wb = w1b[...]
     for a in range(2):
         for b in range(2):
@@ -473,7 +509,7 @@
                     h, 4 * c + 2 * a : 4 * c + 2 * a + 2
                 ].astype(BF16)
 
-    depth_waits, z_waits = [], []
+    depth_waits, y_waits = [], []
 
     @pl.when(second)
     def _():
@@ -483,9 +519,9 @@
 
     @pl.when(first)
     def _():
-        finish(y_waits)
-        s_zr[zh] = summed(s_yr, n_y)
-        z_waits.extend(exchange(s_zr, zh, to_z, z_behind, 0))
+        finish(z_waits)
+        s_yr[y] = summed(s_zr, n_z)
+        y_waits.extend(exchange(s_yr, y, to_y, y_behind, 0))
 
     finish(feat_waits)
     for k in range(n_f):
@@ -494,31 +530,43 @@
 
     @pl.when(first)
     def _():
-        finish(z_waits)
-        s_os[...] = summed(s_zr, n_z)
+        finish(y_waits)
+        s_os[...] = summed(s_yr, n_y)
         send(s_os, s_os, twin, 0)
 
     s_last = len(sent) - 1
+    last_waits = []
 
     @pl.when(second)
     def _():
         finish(depth_waits)
         f_ag[at_xy] = summed(f_zr, 2 * n_z)
-        finish(exchange(f_ag, at_xy, to_plane, plane_behind, 1))
-        send(f_ag, f_ag, twin, 1)
+        waits = exchange(f_ag, at_xy, to_plane, plane_behind, 1)
+        for slot, wait in zip([at_xy] + plane_behind, [None] + waits):
+            if wait is not None:
+                finish([wait])
+
+            def part(slot=slot):
+                return f_ag.at[slot]
+
+            at = send(part(), part(), twin, 1, part)
+            last_waits.append((at, part))
         arrive(s_os, s_last)
 
-    f_last = len(sent) - 1
-
     @pl.when(first)
     def _():
-        arrive(f_ag, f_last)
+        finish(last_waits)
 
     os_out[...] = s_os[...]
     ag_out[...] = f_ag[...]
 
     assert len(sent) <= N_SEMS
     drain(None)
+    for d in DIRS:
+
+        @pl.when(exists[d])
+        def _(d=d):
+            drain(d)
 
     @pl.when(first)
     def _():

time: 54.4 us -> 54.1 us (level)
  no operation moved by 1% of the time
where the time goes in v4:
time: 54.1 us; the launch traced here: 54 us
  Pallas kernels  53.3 us (99%)
  between operations  0.64 us (1%)
    pallas_call x1, Pallas kernels, local(): pl.pallas_call(functools.partial(kernel, sizes), out_shape=(shape((16, 1,...  52.2 us
    pallas_call x1, Pallas kernels, local(): pl.pallas_call(functools.partial(unpack, n_f, scales), out_shape=(shape((...  1.17 us

profile of v4, /device:TPU:1, one launch (start us, length us, event | category | flops | bytes accessed | tf_op | source)
XLA Modules:
  0.0 54.0 jit_solution(5934547681630782188)
XLA Ops:
  0.6 52.2 %block.1 = (bf16[16,1,8,128]{3,2,1,0:T(8,128)(2,1)S(1)}, bf16[64,2,2,256]{3,2,1,0:T(2,128)(2,1)S(1)}, bf16[16,64,128]{2,1,0:T(8,128)(2,1)S(1)}, bf16[256,128]{1,0:T(8,128)(2,1)S(1)}) custom-call(bf16[64,2,2,256]{3,2,1,0:T(2,128)(2,1)} %vol_hbm.1, bf16[16,1,8,128]{3,2,1,0:T(8,128)(2,1)} %cot_hbm.1, bf16[27,64,64]{2,1,0:T(8,128)(2,1)} %w1_hbm.1, ...), custom_call_target="tpu_custom_call" | custom-call | tf_op jit(solution)/shard_map/block/pallas_call | solution.py:617
  52.8 1.2 %unpack.1 = (bf16[16,1,8,128]{3,2,1,0:T(8,128)(2,1)}, bf16[64,2,2,256]{3,2,1,0:T(2,128)(2,1)}, f32[27,64,64]{2,1,0:T(8,128)}, f32[27,16,64]{2,1,0:T(8,128)}) custom-call(bf16[16,1,8,128]{3,2,1,0:T(8,128)(2,1)S(1)} %get-tuple-element.8.feat_in, bf16[64,2,2,256]{3,2,1,0:T(2,128)(2,1)S(1)} %get-tuple-element.9.vgrad_in, ...), custom_call_target="tpu_custom_call" | custom-call | tf_op jit(solution)/shard_map/unpack/pallas_call | solution.py:670

commit v5 on v4

--- a/solution.py
+++ b/solution.py
@@ -11,7 +11,7 @@
 F32 = jnp.float32
 BF16 = jnp.bfloat16
 DIRS = [(-1, -1), (-1, 1), (1, -1), (1, 1), (-1, 0), (1, 0), (0, -1), (0, 1)]
-N_SEMS = 130
+N_SEMS = 34
 
 
 def sigmoid(v):
@@ -134,13 +134,8 @@
     def ahead(me, count):
         return [lax.rem(me + j, count) for j in range(1, count)]
 
-    def behind(me, count):
-        return [lax.rem(me - j + count, count) for j in range(1, count)]
-
-    f_ahead, f_behind = ahead(f, n_f), behind(f, n_f)
-    y_behind, z_behind = behind(y, n_y), behind(zh, n_z)
-    plane_ahead, plane_behind = ahead(at_xy, n_xy), behind(at_xy, n_xy)
-    depth_behind = behind(at_z, 2 * n_z)
+    f_ahead = ahead(f, n_f)
+    plane_ahead = ahead(at_xy, n_xy)
     first, second = core == 0, core == 1
     in_s = {-1: s > 0, 0: s >= 0, 1: s < n_s - 1}
     in_f = {-1: f > 0, 0: f >= 0, 1: f < n_f - 1}
@@ -148,7 +143,6 @@
     beside = {d: near(*d) for d in DIRS}
     flip = (1 - zl) * n_x + x
     x_ahead = [zl * n_x + lax.rem(x + j, n_x) for j in range(1, n_x)]
-    x_behind = [lax.rem(x - j + n_x, n_x) for j in range(1, n_x)]
 
     peers = [beside[d] for d in DIRS] + to_f + to_plane + to_depth
     barrier = pltpu.get_barrier_semaphore()
@@ -170,30 +164,31 @@
                 ].astype(BF16)
     pl.semaphore_wait(barrier, len(peers))
 
-    sent = []
-    groups = {}
-
-    def send(src, dst, device, only=None, size=None):
-        at = len(sent)
-        groups.setdefault(only, []).append((at, size or (lambda: src)))
-        copy = pltpu.make_async_remote_copy(
+    used = []
+    owed = {}
+
+    def fresh(only, size):
+        at = len(used)
+        used.append(at)
+        owed.setdefault(only, []).append((at, size))
+        return at
+
+    def send(src, dst, device, at):
+        pltpu.make_async_remote_copy(
             src_ref=src,
             dst_ref=dst,
             send_sem=send_sem.at[at],
             recv_sem=recv_sem.at[at],
             device_id=device,
             device_id_type=MESH,
-        )
-        copy.start()
-        sent.append(copy)
-        return at
+        ).start()
 
     def arrive(ref, at):
         ref = ref() if callable(ref) else ref
         pltpu.make_async_copy(ref, ref, recv_sem.at[at]).wait()
 
     def drain(only):
-        for at, size in groups[only]:
+        for at, size in owed[only]:
             ref = size()
             pltpu.make_async_copy(ref, ref, send_sem.at[at]).wait()
 
@@ -214,11 +209,13 @@
             def target(dx=dx, dy=dy):
                 return field.at[dst_part(dx), dst_part(dy)]
 
+            at = fresh(d, source)
+
             @pl.when(exists[d])
-            def _(d=d, source=source, target=target):
-                send(source(), target(), beside[d], d, source)
-
-            out.append((d, len(sent) - 1, target))
+            def _(d=d, source=source, target=target, at=at):
+                send(source(), target(), beside[d], at)
+
+            out.append((d, at, target))
         return out
 
     def halo_finish(waits):
@@ -227,10 +224,6 @@
             @pl.when(exists[-dx, -dy])
             def _(at=at, target=target):
                 arrive(target, at)
-
-    def finish(waits):
-        for at, ref in waits:
-            arrive(ref, at)
 
     def zero_rim(field, last):
         @pl.when(s == 0)
@@ -264,22 +257,19 @@
         w2p[k] = side_by_side(w2raw[6 * c + dz], right)
     w2p[15] = jnp.zeros((16, 128), BF16)
     half = w2p.at[pl.ds(8 * core, 8)]
-    w2_flip = send(half, w2g.at[core, f], (s, flip))
-    w2_waits = []
-    for j, to in enumerate(x_ahead):
-        source = zl * n_x + x_behind[j]
-        w2_waits.append((send(half, w2g.at[core, f], (s, to)), w2g.at[core, source]))
+    w2_flip, w2_row = fresh(None, lambda: half), fresh(None, lambda: w2g.at[core, 0 : n_x - 1])
+    send(half, w2g.at[core, f], (s, flip), w2_flip)
+    for to in x_ahead:
+        send(half, w2g.at[core, f], (s, to), w2_row)
     w2g[core, f] = w2p[pl.ds(8 * core, 8)]
 
     loads[2].wait()
     crows[...] = craw[...].reshape(16 * n_f, 128).astype(F32)
     for k in range(n_f):
         cotb[k] = crows[pl.ds(k, 16, stride=n_f), :].astype(BF16)
-    cot_waits = []
-    for j in range(1, n_f):
-        other = lax.rem(f + j, n_f)
-        source = lax.rem(f - j + n_f, n_f)
-        cot_waits.append((send(cotb.at[other], cotg.at[f], along_f(j)), cotg.at[source]))
+    cot_at = fresh(None, lambda: cotb.at[0 : n_f - 1])
+    for other, peer in zip(f_ahead, to_f):
+        send(cotb.at[other], cotg.at[f], peer, cot_at)
     cotg[f] = cotb[f]
 
     loads[3].wait()
@@ -303,10 +293,9 @@
         return jnp.concatenate(planes + [jnp.zeros((64, 256), BF16)], axis=0)
 
     arrive(w2g.at[core, flip], w2_flip)
-    for j, to in enumerate(x_ahead):
-        mine = w2g.at[core, flip]
-        source = (1 - zl) * n_x + x_behind[j]
-        w2_waits.append((send(mine, mine, (s, to)), w2g.at[core, source]))
+    w2_pass = fresh(None, lambda: w2g.at[core, 0 : n_x - 1])
+    for to in x_ahead:
+        send(w2g.at[core, flip], w2g.at[core, flip], (s, to), w2_pass)
     halo_finish(vol_waits)
 
     wf = w1f[...]
@@ -321,15 +310,16 @@
             total = total + jnp.dot(hidden, pairs, preferred_element_type=F32)
     ps[1, 1] = (0.125 * total).astype(BF16)
 
-    pool_waits = []
-    for dx, dy in DIRS:
-        target = ps.at[1 - dx, 1 - dy]
-        pool_waits.append((send(ps.at[1, 1], target, near(dx, dy)), target))
-
-    finish(w2_waits)
-    w2_waits = [(send(w2g.at[core], w2g.at[core], twin), w2g.at[1 - core])]
-    finish(cot_waits)
-    finish(w2_waits)
+    pool_at = fresh(None, lambda: ps.at[0:4, 0:2])
+    for d in DIRS:
+        send(ps.at[1, 1], ps.at[1 - d[0], 1 - d[1]], beside[d], pool_at)
+
+    arrive(lambda: w2g.at[core, 0 : n_x - 1], w2_row)
+    arrive(lambda: w2g.at[core, 0 : n_x - 1], w2_pass)
+    w2_twin = fresh(None, lambda: w2g.at[core])
+    send(w2g.at[core], w2g.at[core], twin, w2_twin)
+    arrive(lambda: cotg.at[0 : n_f - 1], cot_at)
+    arrive(lambda: w2g.at[1 - core], w2_twin)
     w2 = []
     for dz in range(3):
         tiles = [
@@ -339,7 +329,7 @@
         for c in range(5):
             w2t[dz, 128 * c : 128 * c + 128] = tiles[c].astype(F32).T.astype(BF16)
 
-    finish(pool_waits)
+    arrive(lambda: ps.at[0:4, 0:2], pool_at)
     zero_rim(ps, 2)
 
     around = jnp.concatenate(
@@ -353,22 +343,17 @@
 
     rows = [jnp.dot(w2t[dz], down_own, preferred_element_type=F32) for dz in range(3)]
     share = shifted(rows[0], 1) + rows[1] + shifted(rows[2], -1)
-    down_waits = []
+    down_at = fresh(None, lambda: give.at[0:8])
     for dx, dy in DIRS:
         slot = 3 * (dx + 1) + dy + 1
         give[slot] = share[64 * slot : 64 * slot + 64].astype(BF16)
-        target = take.at[1 - dx, 1 - dy]
-        down_waits.append((send(give.at[slot], target, near(dx, dy)), target))
+        send(give.at[slot], take.at[1 - dx, 1 - dy], beside[dx, dy], down_at)
     own_share = share[256:320]
     featb[0] = (pre * gate).astype(BF16).reshape(n_f, 16, 128)
 
-    feat_waits = []
-    for j in range(1, n_f):
-        other = lax.rem(f + j, n_f)
-        source = lax.rem(f - j + n_f, n_f)
-        feat_waits.append(
-            (send(featb.at[0, other], featb.at[1, f], along_f(j)), featb.at[1, source])
-        )
+    feat_at = fresh(None, lambda: featb.at[0, 0 : n_f - 1])
+    for other, peer in zip(f_ahead, to_f):
+        send(featb.at[0, other], featb.at[1, f], peer, feat_at)
     featb[1, f] = featb[0, f]
 
     lhs = jnp.concatenate(
@@ -391,23 +376,21 @@
 
     deal(terms, 16, 16, 128, put_bottom)
 
-    def exchange(ref, mine, peers, sources, only):
-        return [
-            (
-                send(ref.at[mine], ref.at[mine], peer, only, lambda: ref.at[mine]),
-                lambda source=source: ref.at[source],
-            )
-            for peer, source in zip(peers, sources)
-        ]
-
-    def scatter(out, into, mine, peers, theirs, sources, only):
-        return [
-            (
-                send(out.at[other], into.at[mine], peer, only, lambda other=other: out.at[other]),
-                lambda source=source: into.at[source],
-            )
-            for peer, other, source in zip(peers, theirs, sources)
-        ]
+    def exchange(ref, mine, peers, only):
+        at = fresh(only, lambda: ref.at[0 : len(peers)])
+        for peer in peers:
+            send(ref.at[mine], ref.at[mine], peer, at)
+        return at, lambda: ref.at[0 : len(peers)]
+
+    def scatter(out, into, mine, peers, theirs, only):
+        at = fresh(only, lambda: out.at[0 : len(peers)])
+        for peer, other in zip(peers, theirs):
+            send(out.at[other], into.at[mine], peer, at)
+        return at, lambda: into.at[0 : len(peers)]
+
+    def finish(waits):
+        for at, ref in waits:
+            arrive(ref, at)
 
     def summed(ref, count):
         value = ref[0].astype(F32)
@@ -415,22 +398,21 @@
             value = value + ref[k].astype(F32)
         return value.astype(BF16)
 
-    s_waits, f_waits = [], []
+    s_waits = []
+    s_twin = fresh(1, lambda: s_gb)
 
     @pl.when(second)
     def _():
-        send(s_gb, s_cb, twin, 1)
-
-    s_twin = len(sent) - 1
+        send(s_gb, s_cb, twin, s_twin)
 
     @pl.when(first)
     def _():
         arrive(s_cb, s_twin)
         s_pb[...] = (s_gb[...].astype(F32) + s_cb[...].astype(F32)).astype(BF16)
         s_fb[f] = s_pb[f]
-        s_waits.extend(scatter(s_pb, s_fb, f, to_f, f_ahead, f_behind, 0))
-
-    finish(down_waits)
+        s_waits.append(scatter(s_pb, s_fb, f, to_f, f_ahead, 0))
+
+    arrive(lambda: give.at[0:8], down_at)
     zero_rim(take, 2)
     pool_grad = own_share
     for dx, dy in DIRS:
@@ -443,7 +425,6 @@
     for a in range(2):
         for b in range(2):
             extd[a + 1, b + 1] = (spread * slope1[a, b]).astype(BF16)
-    fd_waits = halo_start(extd)
 
     terms = jnp.zeros((192, 640), F32)
     for a in range(2):
@@ -470,28 +451,26 @@
 
         @pl.when(first)
         def _():
-            send(part(f_gb), part(f_cb), twin, 0, lambda: part(f_gb))
-
-        f_twin.append((len(sent) - 1, lambda: part(f_cb)))
-
-    f_twin = []
+            send(part(f_gb), part(f_cb), twin, f_twin)
+
+    f_twin = fresh(0, lambda: f_gb)
     deal(terms, 8, 24, 8, put_fine)
     plane_waits, z_waits = [], []
 
     @pl.when(second)
     def _():
-        finish(f_twin)
+        arrive(f_cb, f_twin)
         f_pb[...] = (f_gb[...].astype(F32) + f_cb[...].astype(F32)).astype(BF16)
         f_xr[at_xy] = f_pb[at_xy]
-        plane_waits.extend(
-            scatter(f_pb, f_xr, at_xy, to_plane, plane_ahead, plane_behind, 1)
-        )
+        plane_waits.append(scatter(f_pb, f_xr, at_xy, to_plane, plane_ahead, 1))
+
+    fd_waits = halo_start(extd)
 
     @pl.when(first)
     def _():
         finish(s_waits)
         s_zr[zh] = summed(s_fb, n_f)
-        z_waits.extend(exchange(s_zr, zh, to_z, z_behind, 0))
+        z_waits.append(exchange(s_zr, zh, to_z, 0))
 
     halo_finish(fd_waits)
     wb = w1b[...]
@@ -515,52 +494,43 @@
     def _():
         finish(plane_waits)
         f_zr[at_z] = summed(f_xr, n_xy)
-        depth_waits.extend(exchange(f_zr, at_z, to_depth, depth_behind, 1))
+        depth_waits.append(exchange(f_zr, at_z, to_depth, 1))
 
     @pl.when(first)
     def _():
         finish(z_waits)
         s_yr[y] = summed(s_zr, n_z)
-        y_waits.extend(exchange(s_yr, y, to_y, y_behind, 0))
-
-    finish(feat_waits)
+        y_waits.append(exchange(s_yr, y, to_y, 0))
+
+    arrive(lambda: featb.at[1, 0 : n_f - 1], feat_at)
     for k in range(n_f):
         crows[pl.ds(k, 16, stride=n_f), :] = featb[1, k].astype(F32)
     feat_out[...] = crows[...].reshape(16, 1, n_f, 128).astype(BF16)
 
+    s_last, f_last = fresh(0, lambda: s_os), fresh(1, lambda: f_ag)
+
     @pl.when(first)
     def _():
         finish(y_waits)
         s_os[...] = summed(s_yr, n_y)
-        send(s_os, s_os, twin, 0)
-
-    s_last = len(sent) - 1
-    last_waits = []
+        send(s_os, s_os, twin, s_last)
 
     @pl.when(second)
     def _():
         finish(depth_waits)
         f_ag[at_xy] = summed(f_zr, 2 * n_z)
-        waits = exchange(f_ag, at_xy, to_plane, plane_behind, 1)
-        for slot, wait in zip([at_xy] + plane_behind, [None] + waits):
-            if wait is not None:
-                finish([wait])
-
-            def part(slot=slot):
-                return f_ag.at[slot]
-
-            at = send(part(), part(), twin, 1, part)
-            last_waits.append((at, part))
+        finish([exchange(f_ag, at_xy, to_plane, 1)])
+        send(f_ag, f_ag, twin, f_last)
         arrive(s_os, s_last)
 
     @pl.when(first)
     def _():
-        finish(last_waits)
+        arrive(f_ag, f_last)
 
     os_out[...] = s_os[...]
     ag_out[...] = f_ag[...]
 
-    assert len(sent) <= N_SEMS
+    assert len(used) <= N_SEMS
     drain(None)
     for d in DIRS:
 

time: 54.1 us -> 53.3 us (0.985)
  Pallas kernels: 53.3 us -> 52.6 us
    pallas_call x1, Pallas kernels: 52.2 us -> 51.4 us  [local(): pl.pallas_call(functools.partial(kernel, sizes), out_shape=(shape((16, 1,...]
where the time goes in v5:
time: 53.3 us
  Pallas kernels  52.6 us (99%)
  between operations  0.64 us (1%)
    pallas_call x1, Pallas kernels, local(): pl.pallas_call(functools.partial(kernel, sizes), out_shape=(shape((16, 1,...  51.4 us
    pallas_call x1, Pallas kernels, local(): pl.pallas_call(functools.partial(unpack, n_f, scales), out_shape=(shape((...  1.17 us

profile of v5, /device:TPU:1, one launch (start us, length us, event | category | flops | bytes accessed | tf_op | source)
XLA Modules:
  0.0 53.3 jit_solution(8387556055336815022)
XLA Ops:
  0.6 51.4 %block.1 = (bf16[16,1,8,128]{3,2,1,0:T(8,128)(2,1)S(1)}, bf16[64,2,2,256]{3,2,1,0:T(2,128)(2,1)S(1)}, bf16[16,64,128]{2,1,0:T(8,128)(2,1)S(1)}, bf16[256,128]{1,0:T(8,128)(2,1)S(1)}) custom-call(bf16[64,2,2,256]{3,2,1,0:T(2,128)(2,1)} %vol_hbm.1, bf16[16,1,8,128]{3,2,1,0:T(8,128)(2,1)} %cot_hbm.1, bf16[27,64,64]{2,1,0:T(8,128)(2,1)} %w1_hbm.1, ...), custom_call_target="tpu_custom_call" | custom-call | tf_op jit(solution)/shard_map/block/pallas_call | solution.py:587
  52.1 1.2 %unpack.1 = (bf16[16,1,8,128]{3,2,1,0:T(8,128)(2,1)}, bf16[64,2,2,256]{3,2,1,0:T(2,128)(2,1)}, f32[27,64,64]{2,1,0:T(8,128)}, f32[27,16,64]{2,1,0:T(8,128)}) custom-call(bf16[16,1,8,128]{3,2,1,0:T(8,128)(2,1)S(1)} %get-tuple-element.8.feat_in, bf16[64,2,2,256]{3,2,1,0:T(2,128)(2,1)S(1)} %get-tuple-element.9.vgrad_in, ...), custom_call_target="tpu_custom_call" | custom-call | tf_op jit(solution)/shard_map/unpack/pallas_call | solution.py:640

commit v6 on v5

--- a/solution.py
+++ b/solution.py
@@ -12,6 +12,15 @@
 BF16 = jnp.bfloat16
 DIRS = [(-1, -1), (-1, 1), (1, -1), (1, 1), (-1, 0), (1, 0), (0, -1), (0, 1)]
 N_SEMS = 34
+
+
+def far_first(*rings):
+    offsets = [()]
+    for length in rings:
+        offsets = [o + (k,) for o in offsets for k in range(length)]
+    hops = [sum(min(k, n - k) for k, n in zip(o, rings)) for o in offsets]
+    order = sorted(range(1, len(offsets)), key=lambda i: -hops[i])
+    return [offsets[i] for i in order]
 
 
 def sigmoid(v):
@@ -101,15 +110,6 @@
     def near(dx, dy):
         return (lax.rem(s + dx + n_s, n_s), lax.rem(f + dy + n_f, n_f))
 
-    def along_f(j):
-        return (s, lax.rem(f + j, n_f))
-
-    def along_y(j):
-        return ((lax.rem(y + j, n_y) * n_z + zh) * 2 + core, f)
-
-    def along_z(j):
-        return ((y * n_z + lax.rem(zh + j, n_z)) * 2 + core, f)
-
     twin = (s + 1 - 2 * core, f)
     n_x = n_f // 2
     n_xy = n_x * n_y
@@ -117,25 +117,27 @@
     at_xy = y * n_x + x
     at_z = 2 * zh + zl
 
-    def over_plane(j):
-        to = lax.rem(at_xy + j, n_xy)
-        return ((to // n_x * n_z + zh) * 2 + core, zl * n_x + lax.rem(to, n_x))
-
-    def over_depth(j):
-        to = lax.rem(at_z + j, 2 * n_z)
-        return ((y * n_z + to // 2) * 2 + core, lax.rem(to, 2) * n_x + x)
-
-    to_f = [along_f(j) for j in range(1, n_f)]
-    to_y = [along_y(j) for j in range(1, n_y)]
-    to_z = [along_z(j) for j in range(1, n_z)]
-    to_plane = [over_plane(j) for j in range(1, n_xy)]
-    to_depth = [over_depth(j) for j in range(1, 2 * n_z)]
-
-    def ahead(me, count):
-        return [lax.rem(me + j, count) for j in range(1, count)]
-
-    f_ahead = ahead(f, n_f)
-    plane_ahead = ahead(at_xy, n_xy)
+    def device(y_to, zh_to, zl_to, x_to):
+        return ((y_to * n_z + zh_to) * 2 + core, zl_to * n_x + x_to)
+
+    def turned_by(position, by, length):
+        return position if by == 0 else lax.rem(position + by, length)
+
+    to_f, f_ahead = [], []
+    for p, q in far_first(2, n_x):
+        to_f.append(device(y, zh, turned_by(zl, p, 2), turned_by(x, q, n_x)))
+        f_ahead.append(to_f[-1][1])
+    to_y = [device(turned_by(y, p, n_y), zh, zl, x) for (p,) in far_first(n_y)]
+    to_z = [device(y, turned_by(zh, p, n_z), zl, x) for (p,) in far_first(n_z)]
+    to_plane, plane_ahead = [], []
+    for p, q in far_first(n_y, n_x):
+        y_to, x_to = turned_by(y, p, n_y), turned_by(x, q, n_x)
+        to_plane.append(device(y_to, zh, zl, x_to))
+        plane_ahead.append(y_to * n_x + x_to)
+    to_depth = []
+    for (p,) in far_first(2 * n_z):
+        to = turned_by(at_z, p, 2 * n_z)
+        to_depth.append(device(y, to // 2, lax.rem(to, 2), x))
     first, second = core == 0, core == 1
     in_s = {-1: s > 0, 0: s >= 0, 1: s < n_s - 1}
     in_f = {-1: f > 0, 0: f >= 0, 1: f < n_f - 1}
@@ -426,6 +428,8 @@
         for b in range(2):
             extd[a + 1, b + 1] = (spread * slope1[a, b]).astype(BF16)
 
+    fd_waits = halo_start(extd)
+
     terms = jnp.zeros((192, 640), F32)
     for a in range(2):
         for b in range(2):
@@ -464,13 +468,25 @@
         f_xr[at_xy] = f_pb[at_xy]
         plane_waits.append(scatter(f_pb, f_xr, at_xy, to_plane, plane_ahead, 1))
 
-    fd_waits = halo_start(extd)
-
     @pl.when(first)
     def _():
         finish(s_waits)
         s_zr[zh] = summed(s_fb, n_f)
         z_waits.append(exchange(s_zr, zh, to_z, 0))
+
+    depth_waits, y_waits = [], []
+
+    @pl.when(second)
+    def _():
+        finish(plane_waits)
+        f_zr[at_z] = summed(f_xr, n_xy)
+        depth_waits.append(exchange(f_zr, at_z, to_depth, 1))
+
+    @pl.when(first)
+    def _():
+        finish(z_waits)
+        s_yr[y] = summed(s_zr, n_z)
+        y_waits.append(exchange(s_yr, y, to_y, 0))
 
     halo_finish(fd_waits)
     wb = w1b[...]
@@ -487,20 +503,6 @@
                 vgrad_out[c, a, :, 128 * h : 128 * h + 128] = vrows[
                     h, 4 * c + 2 * a : 4 * c + 2 * a + 2
                 ].astype(BF16)
-
-    depth_waits, y_waits = [], []
-
-    @pl.when(second)
-    def _():
-        finish(plane_waits)
-        f_zr[at_z] = summed(f_xr, n_xy)
-        depth_waits.append(exchange(f_zr, at_z, to_depth, 1))
-
-    @pl.when(first)
-    def _():
-        finish(z_waits)
-        s_yr[y] = summed(s_zr, n_z)
-        y_waits.append(exchange(s_yr, y, to_y, 0))
 
     arrive(lambda: featb.at[1, 0 : n_f - 1], feat_at)
     for k in range(n_f):

time: 53.3 us -> 50.8 us (0.953)
  Pallas kernels: 52.6 us -> 50 us
    pallas_call x1, Pallas kernels: 51.4 us -> 48.9 us  [local(): pl.pallas_call(functools.partial(kernel, sizes), out_shape=(shape((16, 1,...]
where the time goes in v6:
time: 50.8 us; the launch traced here: 50.7 us
  Pallas kernels  50 us (98%)
  between operations  0.64 us (1%)
    pallas_call x1, Pallas kernels, local(): pl.pallas_call(functools.partial(kernel, sizes), out_shape=(shape((16, 1,...  48.9 us
    pallas_call x1, Pallas kernels, local(): pl.pallas_call(functools.partial(unpack, n_f, scales), out_shape=(shape((...  1.17 us

profile of v6, /device:TPU:1, one launch (start us, length us, event | category | flops | bytes accessed | tf_op | source)
XLA Modules:
  0.0 50.7 jit_solution(4980370738719593304)
XLA Ops:
  0.6 48.9 %block.1 = (bf16[16,1,8,128]{3,2,1,0:T(8,128)(2,1)S(1)}, bf16[64,2,2,256]{3,2,1,0:T(2,128)(2,1)S(1)}, bf16[16,64,128]{2,1,0:T(8,128)(2,1)S(1)}, bf16[256,128]{1,0:T(8,128)(2,1)S(1)}) custom-call(bf16[64,2,2,256]{3,2,1,0:T(2,128)(2,1)} %vol_hbm.1, bf16[16,1,8,128]{3,2,1,0:T(8,128)(2,1)} %cot_hbm.1, bf16[27,64,64]{2,1,0:T(8,128)(2,1)} %w1_hbm.1, ...), custom_call_target="tpu_custom_call" | custom-call | tf_op jit(solution)/shard_map/block/pallas_call | solution.py:589
  49.5 1.2 %unpack.1 = (bf16[16,1,8,128]{3,2,1,0:T(8,128)(2,1)}, bf16[64,2,2,256]{3,2,1,0:T(2,128)(2,1)}, f32[27,64,64]{2,1,0:T(8,128)}, f32[27,16,64]{2,1,0:T(8,128)}) custom-call(bf16[16,1,8,128]{3,2,1,0:T(8,128)(2,1)S(1)} %get-tuple-element.8.feat_in, bf16[64,2,2,256]{3,2,1,0:T(2,128)(2,1)S(1)} %get-tuple-element.9.vgrad_in, ...), custom_call_target="tpu_custom_call" | custom-call | tf_op jit(solution)/shard_map/unpack/pallas_call | solution.py:642

commit v7 on v6

--- a/solution.py
+++ b/solution.py
@@ -307,7 +307,7 @@
             rows = jnp.dot(wf, stack(ext, a, b), preferred_element_type=F32)
             pre = shifted(rows[0:64], -1) + rows[64:128] + shifted(rows[128:192], 1)
             gate = sigmoid(pre)
-            slope1[a, b] = gate * (1.0 + pre * (1.0 - gate))
+            slope1[a, b] = pre
             hidden = (pre * gate).astype(BF16)
             total = total + jnp.dot(hidden, pairs, preferred_element_type=F32)
     ps[1, 1] = (0.125 * total).astype(BF16)
@@ -315,6 +315,12 @@
     pool_at = fresh(None, lambda: ps.at[0:4, 0:2])
     for d in DIRS:
         send(ps.at[1, 1], ps.at[1 - d[0], 1 - d[1]], beside[d], pool_at)
+
+    for a in range(2):
+        for b in range(2):
+            pre = slope1[a, b]
+            gate = sigmoid(pre)
+            slope1[a, b] = gate * (1.0 + pre * (1.0 - gate))
 
     arrive(lambda: w2g.at[core, 0 : n_x - 1], w2_row)
     arrive(lambda: w2g.at[core, 0 : n_x - 1], w2_pass)
@@ -373,8 +379,14 @@
             tiles.append(jnp.zeros((height, 128), F32))
             put(g, jnp.concatenate(tiles, axis=0).astype(BF16))
 
+    s_twin = fresh(1, lambda: s_gb)
+
     def put_bottom(g, piece):
         s_gb[g] = piece
+
+        @pl.when(second)
+        def _():
+            send(s_gb.at[g], s_cb.at[g], twin, s_twin)
 
     deal(terms, 16, 16, 128, put_bottom)
 
@@ -401,12 +413,6 @@
         return value.astype(BF16)
 
     s_waits = []
-    s_twin = fresh(1, lambda: s_gb)
-
-    @pl.when(second)
-    def _():
-        send(s_gb, s_cb, twin, s_twin)
-
     @pl.when(first)
     def _():
         arrive(s_cb, s_twin)

time: 50.8 us -> 50.4 us (level)
  no operation moved by 1% of the time
where the time goes in v7:
time: 50.4 us; the launch traced here: 50.3 us
  Pallas kernels  49.7 us (99%)
  between operations  0.64 us (1%)
    pallas_call x1, Pallas kernels, local(): pl.pallas_call(functools.partial(kernel, sizes), out_shape=(shape((16, 1,...  48.5 us
    pallas_call x1, Pallas kernels, local(): pl.pallas_call(functools.partial(unpack, n_f, scales), out_shape=(shape((...  1.17 us

profile of v7, /device:TPU:1, one launch (start us, length us, event | category | flops | bytes accessed | tf_op | source)
XLA Modules:
  0.0 50.3 jit_solution(3704087523048148972)
XLA Ops:
  0.6 48.5 %block.1 = (bf16[16,1,8,128]{3,2,1,0:T(8,128)(2,1)S(1)}, bf16[64,2,2,256]{3,2,1,0:T(2,128)(2,1)S(1)}, bf16[16,64,128]{2,1,0:T(8,128)(2,1)S(1)}, bf16[256,128]{1,0:T(8,128)(2,1)S(1)}) custom-call(bf16[64,2,2,256]{3,2,1,0:T(2,128)(2,1)} %vol_hbm.1, bf16[16,1,8,128]{3,2,1,0:T(8,128)(2,1)} %cot_hbm.1, bf16[27,64,64]{2,1,0:T(8,128)(2,1)} %w1_hbm.1, ...), custom_call_target="tpu_custom_call" | custom-call | tf_op jit(solution)/shard_map/block/pallas_call | solution.py:595
  49.2 1.2 %unpack.1 = (bf16[16,1,8,128]{3,2,1,0:T(8,128)(2,1)}, bf16[64,2,2,256]{3,2,1,0:T(2,128)(2,1)}, f32[27,64,64]{2,1,0:T(8,128)}, f32[27,16,64]{2,1,0:T(8,128)}) custom-call(bf16[16,1,8,128]{3,2,1,0:T(8,128)(2,1)S(1)} %get-tuple-element.8.feat_in, bf16[64,2,2,256]{3,2,1,0:T(2,128)(2,1)S(1)} %get-tuple-element.9.vgrad_in, ...), custom_call_target="tpu_custom_call" | custom-call | tf_op jit(solution)/shard_map/unpack/pallas_call | solution.py:648
